TPU v7x, 256 devices: a whole 4x4x8 slice. The times are simulated.
256 devices in a mesh: row: 8 (over y, core), col: 16 (over z_lo, x), mp: 2 (over z_hi).
Axes of the slice: x: 4, y: 4, z: 8 (z_hi: 2, z_lo: 4; z = z_hi * 4 + z_lo), core: 2. Of those that a mesh axis runs over, the one named last changes fastest.
Arguments:
- video: bfloat16 [3, 4, 192, 6144], P(None, None, 'row', 'col'), may hold values from -6 to 6
- grad_tokens: bfloat16 [2, 16, 512, 1024], P(None, 'row', 'col', 'mp'), may hold values from -6 to 6
- weight: bfloat16 [3072, 1024], P(None, 'mp'), may hold values from -0.1875 to 0.1875
Outputs:
- video_grad: float32 [3, 4, 192, 6144], P(None, 'mp', 'row', 'col')
- weight_grad: float32 [3072, 1024], P(('row', 'col'), 'mp')
All inputs are finite; a program needn't handle non-finite values.
Results may differ from a plain program's by a relative error of at most 0.0003.
Values may be sent and summed in bfloat16 or wider, within the bound.
A program may use at most 64 MiB of HBM per device.

v0:
```python
import jax
import jax.numpy as jnp
from jax import lax
from jax.sharding import Mesh
from jax.sharding import PartitionSpec as P

ROW = ("row_0", "row_1")
COL = ("col_0", "col_1")
ROW_COL = ("row_0", "row_1", "col_0", "col_1")


def extended_2(cells, sides, width):
    for axis, dim in sides:
        count = lax.axis_size(axis)
        ends = count - 1
        head = lax.slice_in_dim(cells, 0, width, axis=dim)
        tail = lax.slice_in_dim(cells, cells.shape[dim] - width, cells.shape[dim], axis=dim)
        cells = jnp.concatenate(
            [
                lax.ppermute(tail, axis, [(i, (i + 1) % count) for i in range(ends)]),
                cells,
                lax.ppermute(head, axis, [((i + 1) % count, i) for i in range(ends)]),
            ],
            axis=dim,
        )
    return cells


def own_block(parts, axes, turns):
    inside = parts.shape[1:]
    parts = parts.reshape(*(lax.axis_size(a) for a in axes), *inside)
    parts = jnp.moveaxis(parts, turns, range(len(axes))).reshape(-1, *inside)
    for k in turns:
        parts = lax.psum_scatter(parts, axes[k], scatter_dimension=0, tiled=True)
    return parts[0]


def in_blocks(shard, dim, size):
    before, after = (shard.shape[:dim], shard.shape[dim + 1 :])
    return jnp.moveaxis(shard.reshape(*before, size, -1, *after), dim, 0)


def scatter_axes(shard, axes, turns, dim):
    size = lax.axis_size(axes)
    return own_block(in_blocks(shard, dim, size), axes, turns)


def summed_on_arrival(shard, axis, dim):
    parts = in_blocks(shard, dim, lax.axis_size(axis))
    arrived = lax.all_to_all(parts, axis, split_axis=0, concat_axis=0, tiled=True)
    return arrived.sum(axis=0)


def swapped(shard, axis, stride):
    return lax.ppermute(shard, axis, [(i, i ^ 1 << stride) for i in range(lax.axis_size(axis))])


def passed_along(shard, axis, by):
    size = lax.axis_size(axis)
    pairs = [(i, i + by) for i in range(size) if 0 <= i + by < size]
    return lax.ppermute(shard, axis, pairs)


def unfold_axis(ext, axis, count, stride, kernel):
    extra = max(0, 2 * stride - kernel)
    widths = [(0, 0)] * ext.ndim
    widths[axis] = (0, extra)
    ext = jnp.pad(ext, widths)
    lower = lax.slice_in_dim(ext, 0, count * stride, axis=axis)
    upper = lax.slice_in_dim(ext, stride, stride + count * stride, axis=axis)
    shaped = ext.shape[:axis] + (count, stride) + ext.shape[axis + 1 :]
    lower = lower.reshape(shaped)
    upper = lax.slice_in_dim(upper.reshape(shaped), 0, kernel - stride, axis=axis + 1)
    return jnp.concatenate([lower, upper], axis=axis + 1)


def fold_axis(pieces, axis, stride, kernel):
    count = pieces.shape[axis]
    lower = lax.slice_in_dim(pieces, 0, stride, axis=axis + 1)
    upper = lax.slice_in_dim(pieces, stride, kernel, axis=axis + 1)
    pad_lower = [(0, 0)] * pieces.ndim
    pad_upper = [(0, 0)] * pieces.ndim
    pad_lower[axis] = (0, 1)
    pad_upper[axis] = (1, 0)
    pad_upper[axis + 1] = (0, 2 * stride - kernel)
    total = jnp.pad(lower, pad_lower) + jnp.pad(upper, pad_upper)
    merged = total.reshape(pieces.shape[:axis] + ((count + 1) * stride,) + pieces.shape[axis + 2 :])
    return lax.slice_in_dim(merged, 0, count * stride + kernel - stride, axis=axis)


def shards(video, grad_tokens, weight):
    steps, rows, cols, half = grad_tokens.shape
    patch = weight.shape[0]
    parts = lax.axis_size("mp")
    tiles = lax.axis_size(ROW) * lax.axis_size(COL)
    local_steps = steps // parts
    count = steps * rows * cols
    flat = grad_tokens.reshape(count, half)
    framed = extended_2(video, ((ROW, 2), (COL, 3)), 2)
    framed = jnp.pad(framed, ((0, 0), (1, 1), (0, 0), (0, 0)))
    pieces = unfold_axis(framed, 1, steps, 2, 4)
    pieces = unfold_axis(pieces, 3, rows, 12, 16)
    pieces = unfold_axis(pieces, 5, cols, 12, 16)
    patches = pieces.transpose(1, 3, 5, 0, 2, 4, 6).reshape(count, patch)
    block = patches
    summed = scatter_axes(
        lax.dot_general(block, flat, (((0,), (0,)), ((), ())), preferred_element_type=jnp.float32),
        ROW_COL,
        (1, 0, 3, 2),
        0,
    )
    weight_grad = summed * lax.rsqrt(jnp.float32(count * tiles))
    block = flat
    grads = summed_on_arrival(
        lax.dot_general(
            block, weight, (((1,), (1,)), ((), ())), preferred_element_type=jnp.float32
        ),
        "mp",
        0,
    )
    grads = grads.reshape(local_steps, rows, cols, 3, 4, 16, 16).transpose(3, 0, 4, 1, 5, 2, 6)
    grads = fold_axis(grads, 5, 12, 16)
    grads = fold_axis(grads, 3, 12, 16)
    extended = fold_axis(grads, 1, 2, 4)
    first_rim = extended[:, :1]
    last_rim = extended[:, -1:]
    leading = lax.axis_index("mp") == 0
    outgoing = jnp.where(leading, last_rim, first_rim)
    incoming = swapped(outgoing, "mp", 0)
    early = jnp.where(leading, jnp.zeros_like(incoming), incoming)
    late = jnp.where(leading, incoming, jnp.zeros_like(incoming))
    inner = extended[:, 1:-1]
    inner = jnp.concatenate([inner[:, :1] + early, inner[:, 1:-1], inner[:, -1:] + late], axis=1)
    above = passed_along(inner[:, :, -2:], ROW, 1)
    below = passed_along(inner[:, :, :2], ROW, -1)
    middle = inner[:, :, 2:-2]
    middle = jnp.concatenate(
        [middle[:, :, :2] + above, middle[:, :, 2:-2], middle[:, :, -2:] + below], axis=2
    )
    leftward = passed_along(middle[:, :, :, -2:], COL, 1)
    rightward = passed_along(middle[:, :, :, :2], COL, -1)
    center = middle[:, :, :, 2:-2]
    video_grad = jnp.concatenate(
        [center[:, :, :, :2] + leftward, center[:, :, :, 2:-2], center[:, :, :, -2:] + rightward],
        axis=3,
    )
    return (video_grad, weight_grad)


def solution(mesh):
    finer = Mesh(
        mesh.devices.reshape(4, 2, 4, 4, mesh.shape["mp"]),
        ("row_0", "row_1", "col_0", "col_1", "mp"),
    )
    return jax.shard_map(
        shards,
        mesh=finer,
        in_specs=(P(None, None, ROW, COL), P(None, ROW, COL, "mp"), P(None, "mp")),
        out_specs=(P(None, "mp", ROW, COL), P(ROW_COL, "mp")),
        check_vma=False,
    )
```

profile of v0, /device:TPU:2, one launch (start us, length us, event | category | flops | bytes accessed | tf_op | source)
XLA Modules:
  0.0 269.8 jit_solution(6178385522202980938)
XLA Ops:
  7.2 1.1 fusion.17
  8.3 1.7 collective-permute-start.5
  10.1 1.3 collective-permute-start.6
  11.4 3.1 %collective-permute-done.6 = bf16[3,4,2,384]{3,2,1,0:T(2,128)(2,1)S(1)} collective-permute-done((bf16[3,4,2,384]{3,2,1,0:T(2,128)(2,1)S(1)}, bf16[3,4,2,384]{3,2,1,0:T(2,128)(2,1)S(1)}, u32[]{:S(2)}, u32[]{:S(2)}) %collective-permute-start.6) | collective-permute-done | bytes 18464 | tf_op jit(solution)/shard_map/ppermute | solution.py:22
  14.5 1.0 pad_maximum_fusion.6
  15.6 3.4 %collective-permute-start.7 = (bf16[3,4,28,2]{3,2,1,0:T(8,128)(2,1)S(1)}, bf16[3,4,28,2]{3,2,1,0:T(8,128)(2,1)S(1)}, u32[]{:S(2)}, u32[]{:S(2)}) collective-permute-start(bf16[3,4,28,2]{3,2,1,0:T(8,128)(2,1)S(1)} %get-tuple-element.16), channel_id=1, source_target_pairs={{0,2},{2,4},{4,6},{6,8},{8,10},{10,12},{12,14},{14,16},{16,18},{18... | collective-permute-start | bytes 4040 | tf_op jit(solution)/shard_map/ppermute | solution.py:20
  19.0 2.4 collective-permute-start.8
  21.4 0.7 collective-permute-done.7
  22.1 3.4 %collective-permute-done.8 = bf16[3,4,28,2]{3,2,1,0:T(8,128)(2,1)S(1)} collective-permute-done((bf16[3,4,28,2]{3,2,1,0:T(8,128)(2,1)S(1)}, bf16[3,4,28,2]{3,2,1,0:T(8,128)(2,1)S(1)}, u32[]{:S(2)}, u32[]{:S(2)}) %collective-permute-start.8) | collective-permute-done | bytes 1376 | tf_op jit(solution)/shard_map/ppermute | solution.py:22
  25.5 1.3 select_maximum_fusion
  26.9 0.4 copy.26
  27.3 0.4 copy.27
  27.6 0.8 pad_maximum_fusion.1
  28.4 0.7 fusion.3
  29.1 0.2 pad_slice_fusion.1
  29.4 0.5 pad_maximum_fusion
  29.9 1.2 fusion.4
  31.1 0.6 pad_slice_fusion.2
  31.7 0.9 copy.29
  32.6 16.3 %reshape.58 = bf16[3,2,4,2,16,32,12]{6,5,4,3,2,1,0:T(8,128)(2,1)} reshape(bf16[3,2,4,2,16,384]{5,4,3,2,1,0:T(8,128)(2,1)} %copy.29) | data formatting | bytes 1179648 | tf_op jit(solution)/shard_map/reshape | solution.py:73
  48.9 2.0 copy.28
  50.9 16.3 %reshape.57 = bf16[3,2,4,2,16,32,12]{6,5,4,3,2,1,0:T(8,128)(2,1)} reshape(bf16[3,2,4,2,16,384]{5,4,3,2,1,0:T(8,128)(2,1)} %copy.28) | data formatting | bytes 1179648 | tf_op jit(solution)/shard_map/reshape | solution.py:72
  67.2 9.6 %maximum_bitcast_fusion = bf16[2,2,32,3,4,16,16]{6,2,5,1,4,0,3:T(8,128)(2,1)} fusion(bf16[3,2,4,2,16,32,4]{6,5,4,3,2,1,0:T(8,128)(2,1)} %bitcast.43, bf16[3,2,4,2,16,32,12]{6,5,4,3,2,1,0:T(8,128)(2,1)} %reshape.57), kind=kLoop, calls=%fused_computation | loop fusion | flops 1572864 | bytes 1572864 | tf_op jit(solution)/shard_map/transpose | solution.py:104
  76.9 9.7 %copy.30 = bf16[2,2,32,3,4,16,16]{2,1,0,6,5,4,3:T(2,128)(2,1)} copy(bf16[2,2,32,3,4,16,16]{6,2,5,1,4,0,3:T(8,128)(2,1)} %maximum_bitcast_fusion) | data formatting | bytes 1572864 | tf_op jit(solution)/shard_map/transpose | solution.py:104
  86.6 7.0 %reshape.59 = bf16[128,3072]{0,1:T(8,128)(2,1)} reshape(bf16[2,2,32,3,4,16,16]{2,1,0,6,5,4,3:T(2,128)(2,1)} %copy.30) | data formatting | bytes 1572864 | tf_op jit(solution)/shard_map/reshape | solution.py:104
  93.5 2.1 convolution_bitcast_fusion
  95.6 3.4 %copy.31 = f32[2,4,4,4,24,512]{5,4,3,2,1,0:T(8,128)} copy(f32[2,4,4,4,24,512]{5,4,2,3,0,1:T(8,128)S(1)} %convolution_bitcast_fusion) | data formatting | bytes 12582912 | tf_op jit(solution)/shard_map/transpose | solution.py:32
  99.1 26.3 %reduce-scatter.5.cloned.1.call-done = f32[64,24,512]{2,1,0:T(8,128)} async-done(((f32[128,24,512]{2,1,0:T(8,128)}), f32[64,24,512]{2,1,0:T(8,128)}) %reduce-scatter.5.cloned.1.call-update) | async-done | bytes 3145744 | tf_op jit(solution)/shard_map/reduce_scatter | solution.py:34
  125.5 2.3 fusion
  127.8 7.0 %all-to-all-start = ((f32[2,64,3072]{2,1,0:T(8,128)}), f32[2,64,3072]{2,1,0:T(8,128)}, u32[]{:S(2)}, u32[]{:S(2)}) async-start(f32[2,64,3072]{2,1,0:T(8,128)} %fusion), calls=%async_computation | async-start | bytes 3145728 | tf_op jit(solution)/shard_map/all_to_all | solution.py:50
  134.8 38.1 %all-to-all-done = f32[2,64,3072]{2,1,0:T(8,128)} async-done(((f32[2,64,3072]{2,1,0:T(8,128)}), f32[2,64,3072]{2,1,0:T(8,128)}, u32[]{:S(2)}, u32[]{:S(2)}) %all-to-all-start) | async-done | bytes 1572896 | tf_op jit(solution)/shard_map/all_to_all | solution.py:50
  172.9 2.5 reduce_sum.9
  175.4 2.8 %copy.22 = f32[64,3072]{0,1:T(8,128)} copy(f32[64,3072]{1,0:T(8,128)} %reduce_sum.9) | data formatting | bytes 1572864 | tf_op jit(solution)/shard_map/reduce_sum | solution.py:51
  178.2 4.1 %reshape.49 = f32[1,2,32,3,4,16,16]{2,1,6,5,4,3,0:T(2,128)} reshape(f32[64,3072]{0,1:T(8,128)} %copy.22) | data formatting | bytes 1572864 | tf_op jit(solution)/shard_map/reshape | solution.py:121
  182.3 2.7 slice.147
  185.0 1.4 slice.148
  186.4 3.1 %pad_add_fusion = f32[3,1,4,2,16,33,12]{5,3,6,4,2,0,1:T(2,128)} fusion(f32[3,1,4,2,16,32,4]{5,3,6,4,2,0,1:T(2,128)S(1)} %slice.148, f32[3,1,4,2,16,32,12]{5,3,6,4,2,0,1:T(2,128)S(1)} %slice.147), kind=kLoop, calls=%fused_computation.4 | loop fusion | flops 152064 | bytes 1394688 | tf_op jit(solution)/shard_map/add | solution.py:86
  189.5 7.3 %copy.23 = f32[3,1,4,2,16,33,12]{6,5,4,3,2,0,1:T(8,128)} copy(f32[3,1,4,2,16,33,12]{5,3,6,4,2,0,1:T(2,128)} %pad_add_fusion) | data formatting | bytes 1216512 | tf_op jit(solution)/shard_map/add | solution.py:86
  196.9 5.6 %reshape.50 = f32[3,1,4,2,16,396]{5,4,3,2,0,1:T(8,128)} reshape(f32[3,1,4,2,16,33,12]{6,5,4,3,2,0,1:T(8,128)} %copy.23) | data formatting | bytes 1216512 | tf_op jit(solution)/shard_map/reshape | solution.py:87
  202.5 1.0 slice.150
  203.5 1.3 pad_add_fusion.1
  204.8 0.6 copy.24
  205.4 1.0 fusion.15
  206.4 1.2 pad_add_fusion.2
  207.7 1.1 copy.25
  208.8 2.6 reshape.52
  211.4 1.6 broadcast_select_fusion.2
  213.0 11.1 %collective-permute-done = f32[3,1,28,388]{3,1,2,0:T(1,128)S(1)} collective-permute-done((f32[3,1,28,388]{3,1,2,0:T(1,128)S(1)}, f32[3,1,28,388]{3,1,2,0:T(1,128)S(1)}, u32[]{:S(2)}, u32[]{:S(2)}) %collective-permute-start) | collective-permute-done | bytes 130400 | tf_op jit(solution)/shard_map/ppermute | solution.py:55
  224.2 1.8 fusion.11
  226.0 1.3 collective-permute-start.1
  227.3 0.8 collective-permute-done.1
  228.2 1.3 collective-permute-start.2
  229.5 0.2 fusion.10
  229.7 3.3 %collective-permute-done.2 = f32[3,2,2,388]{3,1,2,0:T(2,128)S(1)} collective-permute-done((f32[3,2,2,388]{3,1,2,0:T(2,128)S(1)}, f32[3,2,2,388]{3,1,2,0:T(2,128)S(1)}, u32[]{:S(2)}, u32[]{:S(2)}) %collective-permute-start.2) | collective-permute-done | bytes 18656 | tf_op jit(solution)/shard_map/ppermute | solution.py:61
  233.4 3.3 %collective-permute-start.3 = (f32[3,2,24,2]{3,1,2,0:T(2,128)S(1)}, f32[3,2,24,2]{3,1,2,0:T(2,128)}, u32[]{:S(2)}, u32[]{:S(2)}) collective-permute-start(f32[3,2,24,2]{3,1,2,0:T(2,128)S(1)} %slice.162), channel_id=1, source_target_pairs={{0,2},{2,4},{4,6},{6,8},{8,10},{10,12},{12,14},{14,16},{16,18},{18... | collective-permute-start | bytes 3464 | tf_op jit(solution)/shard_map/ppermute | solution.py:61
  236.8 2.9 %collective-permute-done.3 = f32[3,2,24,2]{3,1,2,0:T(2,128)} collective-permute-done((f32[3,2,24,2]{3,1,2,0:T(2,128)S(1)}, f32[3,2,24,2]{3,1,2,0:T(2,128)}, u32[]{:S(2)}, u32[]{:S(2)}) %collective-permute-start.3) | collective-permute-done | bytes 1184 | tf_op jit(solution)/shard_map/ppermute | solution.py:61
  239.8 1.0 slice_add_fusion.1
  240.8 1.9 collective-permute-start.4
  242.7 0.3 slice.163
  243.0 4.0 %collective-permute-done.4 = f32[3,2,24,2]{3,1,2,0:T(2,128)S(1)} collective-permute-done((f32[3,2,24,2]{3,1,2,0:T(2,128)S(1)}, f32[3,2,24,2]{3,1,2,0:T(2,128)S(1)}, u32[]{:S(2)}, u32[]{:S(2)}) %collective-permute-start.4) | collective-permute-done | bytes 1184 | tf_op jit(solution)/shard_map/ppermute | solution.py:61
  247.1 0.4 pad_maximum_fusion.3
  247.5 0.7 copy.32
  248.2 13.7 %reduce-scatter.11.cloned.1.call-done = f32[1,24,512]{2,1,0:T(8,128)} async-done(((f32[4,24,512]{2,1,0:T(8,128)}), f32[1,24,512]{2,1,0:T(8,128)}) %reduce-scatter.11.cloned.1.call-update) | async-done | bytes 49168 | tf_op jit(solution)/shard_map/reduce_scatter | solution.py:34
  261.8 1.4 multiply_bitcast_fusion
  (24 shorter events, 0.9 us)
Async XLA Ops:
  7.2 118.3 %copy-start = (bf16[3072,512]{1,0:T(8,128)(2,1)S(1)}, bf16[3072,512]{1,0:T(8,128)(2,1)}, u32[]{:S(2)}) copy-start(bf16[3072,512]{1,0:T(8,128)(2,1)} %param.5) | copy-start | bytes 9437188
  7.2 118.3 %reduce-scatter.5.cloned.1.call-start = ((), (), s32[]{:S(2)}) async-start(), calls=%async_computation.5 | async-start | bytes 9437184 | tf_op jit(solution)/shard_map/reduce_scatter | solution.py:34
  8.3 3.1 %collective-permute-start.5 = (bf16[3,4,2,384]{3,2,1,0:T(2,128)(2,1)S(1)}, bf16[3,4,2,384]{3,2,1,0:T(2,128)(2,1)S(1)}, u32[]{:S(2)}, u32[]{:S(2)}) collective-permute-start(bf16[3,4,2,384]{3,2,1,0:T(2,128)(2,1)S(1)} %get-tuple-element.18), channel_id=1, source_target_pairs={{0,32},{32,64},{64,96},{96,128},{128,160},{160,192},{192,224},{1,3... | collective-permute-start | bytes 55304 | tf_op jit(solution)/shard_map/ppermute | solution.py:20
  10.1 4.4 %collective-permute-start.6 = (bf16[3,4,2,384]{3,2,1,0:T(2,128)(2,1)S(1)}, bf16[3,4,2,384]{3,2,1,0:T(2,128)(2,1)S(1)}, u32[]{:S(2)}, u32[]{:S(2)}) collective-permute-start(bf16[3,4,2,384]{3,2,1,0:T(2,128)(2,1)S(1)} %get-tuple-element.19), channel_id=1, source_target_pairs={{32,0},{64,32},{96,64},{128,96},{160,128},{192,160},{224,192},{33,... | collective-permute-start | bytes 55304 | tf_op jit(solution)/shard_map/ppermute | solution.py:22
  15.6 6.5 %collective-permute-start.7 = (bf16[3,4,28,2]{3,2,1,0:T(8,128)(2,1)S(1)}, bf16[3,4,28,2]{3,2,1,0:T(8,128)(2,1)S(1)}, u32[]{:S(2)}, u32[]{:S(2)}) collective-permute-start(bf16[3,4,28,2]{3,2,1,0:T(8,128)(2,1)S(1)} %get-tuple-element.16), channel_id=1, source_target_pairs={{0,2},{2,4},{4,6},{6,8},{8,10},{10,12},{12,14},{14,16},{16,18},{18... | collective-permute-start | bytes 4040 | tf_op jit(solution)/shard_map/ppermute | solution.py:20
  19.0 6.5 %collective-permute-start.8 = (bf16[3,4,28,2]{3,2,1,0:T(8,128)(2,1)S(1)}, bf16[3,4,28,2]{3,2,1,0:T(8,128)(2,1)S(1)}, u32[]{:S(2)}, u32[]{:S(2)}) collective-permute-start(bf16[3,4,28,2]{3,2,1,0:T(8,128)(2,1)S(1)} %get-tuple-element.17), channel_id=1, source_target_pairs={{2,0},{4,2},{6,4},{8,6},{10,8},{12,10},{14,12},{16,14},{18,16},{20... | collective-permute-start | bytes 4040 | tf_op jit(solution)/shard_map/ppermute | solution.py:22
  86.6 7.0 %copy-start.1 = (bf16[2,2,32,512]{3,2,1,0:T(8,128)(2,1)S(1)}, bf16[2,2,32,512]{3,2,1,0:T(8,128)(2,1)}, u32[]{:S(2)}) copy-start(bf16[2,2,32,512]{3,2,1,0:T(8,128)(2,1)} %param.4) | copy-start | bytes 393220
  99.0 107.3 %reduce-scatter.7.cloned.1.call-start = ((), (), s32[]{:S(2)}) async-start(), calls=%async_computation.6 | async-start | bytes 3932160 | tf_op jit(solution)/shard_map/reduce_scatter | solution.py:34
  127.8 45.2 %all-to-all-start = ((f32[2,64,3072]{2,1,0:T(8,128)}), f32[2,64,3072]{2,1,0:T(8,128)}, u32[]{:S(2)}, u32[]{:S(2)}) async-start(f32[2,64,3072]{2,1,0:T(8,128)} %fusion), calls=%async_computation | async-start | bytes 3145728 | tf_op jit(solution)/shard_map/all_to_all | solution.py:50
  134.8 102.0 %reduce-scatter.9.cloned.1.call-start = ((), (), s32[]{:S(2)}) async-start(), calls=%async_computation.7 | async-start | bytes 983040 | tf_op jit(solution)/shard_map/reduce_scatter | solution.py:34
  206.4 55.4 %reduce-scatter.11.cloned.1.call-start = ((), (), s32[]{:S(2)}) async-start(), calls=%async_computation.8 | async-start | bytes 245760 | tf_op jit(solution)/shard_map/reduce_scatter | solution.py:34
  212.9 11.2 %collective-permute-start = (f32[3,1,28,388]{3,1,2,0:T(1,128)S(1)}, f32[3,1,28,388]{3,1,2,0:T(1,128)S(1)}, u32[]{:S(2)}, u32[]{:S(2)}) collective-permute-start(f32[3,1,28,388]{3,1,2,0:T(1,128)S(1)} %broadcast_select_fusion.2), channel_id=1, source_target_pairs={{0,1},{1,0},{2,3},{3,2},{4,5},{5,4},{6,7},{7,6},{8,9},{9,8},{10,11... | collective-permute-start | bytes 391112 | tf_op jit(solution)/shard_map/ppermute | solution.py:55
  226.0 2.1 collective-permute-start.1
  228.2 4.9 %collective-permute-start.2 = (f32[3,2,2,388]{3,1,2,0:T(2,128)S(1)}, f32[3,2,2,388]{3,1,2,0:T(2,128)S(1)}, u32[]{:S(2)}, u32[]{:S(2)}) collective-permute-start(f32[3,2,2,388]{3,1,2,0:T(2,128)S(1)} %get-tuple-element.13), channel_id=1, source_target_pairs={{32,0},{64,32},{96,64},{128,96},{160,128},{192,160},{224,192},{33,... | collective-permute-start | bytes 55880 | tf_op jit(solution)/shard_map/ppermute | solution.py:61
  233.4 6.4 %collective-permute-start.3 = (f32[3,2,24,2]{3,1,2,0:T(2,128)S(1)}, f32[3,2,24,2]{3,1,2,0:T(2,128)}, u32[]{:S(2)}, u32[]{:S(2)}) collective-permute-start(f32[3,2,24,2]{3,1,2,0:T(2,128)S(1)} %slice.162), channel_id=1, source_target_pairs={{0,2},{2,4},{4,6},{6,8},{8,10},{10,12},{12,14},{14,16},{16,18},{18... | collective-permute-start | bytes 3464 | tf_op jit(solution)/shard_map/ppermute | solution.py:61
  240.8 6.2 %collective-permute-start.4 = (f32[3,2,24,2]{3,1,2,0:T(2,128)S(1)}, f32[3,2,24,2]{3,1,2,0:T(2,128)S(1)}, u32[]{:S(2)}, u32[]{:S(2)}) collective-permute-start(f32[3,2,24,2]{3,1,2,0:T(2,128)S(1)} %get-tuple-element.15), channel_id=1, source_target_pairs={{2,0},{4,2},{6,4},{8,6},{10,8},{12,10},{14,12},{16,14},{18,16},{20... | collective-permute-start | bytes 3464 | tf_op jit(solution)/shard_map/ppermute | solution.py:61
Sparse Core Ops, SparseCore 0:
  99.2 26.2 reduce-scatter.4
  128.0 42.1 reduce-scatter.6
  206.5 20.5 reduce-scatter.8
  236.9 24.8 reduce-scatter.10
where the time goes:
time: 271 us; the launch traced here: 270 us
  waiting for transfers between devices  108 us (40%)
  local copies, waits for them, and re-layouts  89.7 us (33%)
  other arithmetic  30 us (11%)
  starting transfers between devices  23.9 us (9%)
  between operations  14 us (5%)
  matrix products  4.38 us (2%)
    reduce_scatter x4, waiting for transfers between devices, own_block(): parts = lax.psum_scatter(parts, axes[k], scatter_dimension=0, tiled=True)  40 us
    all_to_all x1, waiting for transfers between devices, summed_on_arrival(): lax.all_to_all(parts, axis, split_axis=0, concat_axis=0, tiled=True)  38.1 us
    reshape x2, local copies, waits for them, and re-layouts, unfold_axis(): lower = lower.reshape(shaped)  16.7 us
    reshape x2, local copies, waits for them, and re-layouts, unfold_axis(): upper.reshape(shaped)  16.7 us
    ppermute x4, waiting for transfers between devices, passed_along(): return lax.ppermute(shard, axis, pairs)  11.1 us
    ppermute x1, waiting for transfers between devices, swapped(): lax.ppermute(shard, axis, [(i, i ^ 1 << stride) for i in range(lax.axis_s...  11.1 us
    transpose x1, local copies, waits for them, and re-layouts, shards(): patches = pieces.transpose(1, 3, 5, 0, 2, 4, 6).reshape(count, patch)  9.68 us
    transpose x1, other arithmetic, shards(): patches = pieces.transpose(1, 3, 5, 0, 2, 4, 6).reshape(count, patch)  9.64 us
  transfers between devices with their start and end apart: 14, of which 11 were waited for; matrix products, arithmetic and copies ran while one was open for 17% of the time, Pallas kernels for 0%

commit v1 on v0

v1 whole, which is shorter than its diff:
```python
import jax
import jax.numpy as jnp
import numpy as np
from jax import lax
from jax.experimental import pallas as pl
from jax.experimental.pallas import tpu as pltpu
from jax.sharding import PartitionSpec as P

MESH = pl.DeviceIdType.MESH
F32 = jnp.float32
BF16 = jnp.bfloat16
N_SEMS = 37


def selections():
    cols = np.zeros((384, 512), np.float32)
    for e in range(16):
        for j in range(32):
            x = 12 * j + e - 2
            if 0 <= x < 384:
                cols[x, e * 32 + j] = 1
    side = np.zeros((32, 512), np.float32)
    side[2, 0] = side[3, 32] = 1
    side[16, 14 * 32 + 31] = side[17, 15 * 32 + 31] = 1
    rows = np.zeros((384, 384), np.float32)
    for cf in range(12):
        for i in range(2):
            for b in range(16):
                y = 12 * i + b - 2
                src = cf * 24 + y if 0 <= y < 24 else 288 + cf * 2 + y + 2 if y < 0 else 320 + cf * 2 + y - 24
                rows[cf * 32 + i * 16 + b, src] = 1
    pick = np.zeros((16, 384), np.float32)
    for k, x in enumerate((0, 1, 382, 383)):
        pick[k, x] = 1
    rim = np.zeros((64, 288), np.float32)
    for cf in range(12):
        for k in range(2):
            rim[cf * 2 + k, cf * 24 + 22 + k] = 1
            rim[32 + cf * 2 + k, cf * 24 + k] = 1
    ends = np.zeros((16, 128), np.float32)
    for ti in range(4):
        ends[ti, ti * 32] = 1
        ends[4 + ti, ti * 32 + 31] = 1
    beside = np.zeros((256, 128), np.float32)
    for t in range(2):
        for i4 in range(4):
            i = (1, 0, 1, 0)[i4]
            left = (2, 0, 0, 3)[i4]
            right = (4, 1, 1, 5)[i4]
            beside[t * 128 + i4 * 32, left * 16 + 4 + t * 2 + i] = 1
            beside[t * 128 + i4 * 32 + 31, right * 16 + t * 2 + i] = 1
    back = np.zeros((384, 384), np.float32)
    for e in range(12):
        for j in range(32):
            back[e * 32 + j, 12 * j + e] = 1
    return [cols, side, rows, pick, rim, ends, beside, back]


def chosen(at, values):
    out = jnp.int32(values[3])
    for k in range(3):
        out = jnp.where(at == k, jnp.int32(values[k]), out)
    return out


FRAMES_OF = ((0, 1, 2, 3), (2, 4, 5, 6), (5, 6, 7, 9), (8, 9, 10, 11))
SLOTS_OF = (
    (((4, 0, 1), (1, 2, 3))),
    (((0, 4, 1), (4, 2, 3))),
    (((0, 1, 4), (2, 4, 3))),
    (((0, 1, 2), (2, 3, 4))),
)


def dot(a, b, dims=((1,), (0,))):
    return lax.dot_general(a, b, (dims, ((), ())), preferred_element_type=F32)


def kernel(
    video, tokens, weight, cols_h, side_h, rows_h, pick_h, rim_h, ends_h, beside_h, back_h,
    vout, wout,
    cols, side, rows, pick, rim, ends, beside, back,
    wv, vs, hv, he, sb, hs, gx, ge, gbuf, qs, qw, sq, qr, rq, lm, pg, fs, ll, vg, mr,
    wg, cr, a1, xa, xb, xr1, xr2, xs1, xs2, a2, zr,
    load, send, recv,
):
    r = lax.axis_index("row")
    c = lax.axis_index("col")
    m = lax.axis_index("mp")
    y, core = r // 2, r % 2
    z, x = c // 4, c % 4

    pairs = [
        (video, vs.at[0:288]), (rim_h, rim), (pick_h, pick), (tokens, gx.at[:, 1:3]), (ends_h, ends),
        (tokens, gbuf.at[:, 0]), (cols_h, cols), (side_h, side), (rows_h, rows),
        (beside_h, beside), (back_h, back), (weight, wv),
    ]
    loads = [pltpu.make_async_copy(a, b, load.at[k]) for k, (a, b) in enumerate(pairs)]
    for one in loads:
        one.start()

    hv[...] = jnp.zeros_like(hv)
    he[...] = jnp.zeros_like(he)
    vs[288:384, :] = jnp.zeros((96, 384), BF16)
    for i4 in (0, 3):
        gx[:, i4] = jnp.zeros((2, 32, 512), BF16)
    lm[4] = jnp.zeros((16, 16, 256), BF16)

    barrier = pltpu.get_barrier_semaphore()
    up, down, lef, rig = r > 0, r < 7, c > 0, c < 15
    near = [
        (up, {"row": r - 1}), (down, {"row": r + 1}), (lef, {"col": c - 1}), (rig, {"col": c + 1}),
        (up & lef, {"row": r - 1, "col": c - 1}), (up & rig, {"row": r - 1, "col": c + 1}),
        (down & lef, {"row": r + 1, "col": c - 1}), (down & rig, {"row": r + 1, "col": c + 1}),
    ]
    yp, ym = {"row": (r + 2) % 8}, {"row": (r + 6) % 8}
    xp, xm = {"col": z * 4 + (x + 1) % 4}, {"col": z * 4 + (x + 3) % 4}
    other = {"row": y * 2 + 1 - core}
    zs = [{"col": ((z + d) % 4) * 4 + x} for d in (1, 2, 3)]
    partner = {"mp": 1 - m}

    def greet(to):
        pl.semaphore_signal(barrier, inc=1, device_id=to, device_id_type=MESH)

    for to in (yp, ym, xp, xm, other, *zs, partner):
        greet(to)
    for there, to in near:
        pl.when(there)(lambda to=to: greet(to))

    def one_if(p):
        return jnp.where(p, jnp.int32(1), jnp.int32(0))

    n_near = (1 + one_if(up) + one_if(down)) * (1 + one_if(lef) + one_if(rig)) - 1

    def remote(k, src, dst, to):
        return pltpu.make_async_remote_copy(
            src_ref=src, dst_ref=dst, send_sem=send.at[k], recv_sem=recv.at[k],
            device_id=to, device_id_type=MESH,
        )

    for k in range(5):
        loads[k].wait()
    vs[288:352, :] = dot(rim[...], vs[0:288, :]).astype(BF16)
    sb[:, 384:896] = dot(ends[...], gx[:, 1:3].reshape(128, 512)).astype(BF16)
    sb[:, 0:384] = dot(pick[...], vs[...], ((1,), (1,))).astype(BF16)
    loads[5].wait()

    pl.semaphore_wait(barrier, 9 + n_near)

    halo = [
        (remote(2, vs.at[288:320], hv.at[0:32], {"row": r + 1}), down, up),
        (remote(3, vs.at[320:352], hv.at[32:64], {"row": r - 1}), up, down),
        (remote(4, sb, he.at[0], {"col": c + 1}), rig, lef),
        (remote(5, sb, he.at[1], {"col": c - 1}), lef, rig),
        (remote(6, sb, he.at[2], {"row": r + 1, "col": c + 1}), down & rig, up & lef),
        (remote(7, sb, he.at[3], {"row": r - 1, "col": c + 1}), up & rig, down & lef),
        (remote(8, sb, he.at[4], {"row": r + 1, "col": c - 1}), down & lef, up & rig),
        (remote(9, sb, he.at[5], {"row": r - 1, "col": c - 1}), up & lef, down & rig),
        (remote(0, gx.at[:, 1], gx.at[:, 3], {"row": r - 1}), up, down),
        (remote(1, gx.at[:, 2], gx.at[:, 0], {"row": r + 1}), down, up),
    ]
    for copy, sent, _ in halo[:8]:
        pl.when(sent)(lambda copy=copy: copy.start())
    g_p = remote(16, gbuf.at[:, 0], gbuf.at[:, 1], yp)
    g_m = remote(17, gbuf.at[:, 0], gbuf.at[:, 2], ym)
    g_p.start()
    g_m.start()
    for copy, sent, _ in halo[8:]:
        pl.when(sent)(lambda copy=copy: copy.start())

    for k in (6, 7, 8):
        loads[k].wait()
    for copy, _, got in halo[:8]:
        pl.when(got)(lambda copy=copy: copy.wait_recv())
    lane = lax.broadcasted_iota(jnp.int32, (16, 128), 1)
    for k, (a, b, d) in enumerate(((0, 2, 3), (1, 4, 5))):
        hs[16 * k : 16 * k + 16, 0:256] = he[a, :, 0:256]
        tile = jnp.where(
            lane < 32, he[a, :, 256:384].astype(F32),
            jnp.where(lane < 64, he[b, :, 256:384].astype(F32), he[d, :, 256:384].astype(F32)),
        )
        hs[16 * k : 16 * k + 16, 256:384] = tile.astype(BF16)
    from_side = dot(hs[...], side[...], ((0,), (0,)))
    qs[0:288, :] = (dot(vs[0:288, :], cols[...]) + from_side[0:288]).astype(BF16)
    qs[288:384, :] = (dot(hv[...], cols[...]) + from_side[288:384]).astype(BF16)
    qw[...] = dot(rows[...], qs[...]).astype(BF16).reshape(12, 2, 16, 512)

    for d, to in ((2, 2), (0, 1), (1, 3)):
        for s in range(4):
            at = chosen((y + to) % 4, [f[s] for f in FRAMES_OF])
            sq[d, :, s] = qw[at]
    q_far_p = remote(22, sq.at[2, :, 0:2], rq.at[0], yp)
    q_far_m = remote(23, sq.at[2, :, 2:4], rq.at[1], ym)
    q_p = remote(20, sq.at[0], qr.at[1], yp)
    q_m = remote(21, sq.at[1], qr.at[2], ym)
    for one in (q_far_p, q_far_m, q_p, q_m):
        one.start()
    for s in range(4):
        at = chosen(y, [f[s] for f in FRAMES_OF])
        qr[0, :, s] = qw[at]

    g_p.wait_recv()
    gf_p = remote(18, gbuf.at[0, 1], gbuf.at[0, 3], yp)
    gf_p.start()
    g_m.wait_recv()
    gf_m = remote(19, gbuf.at[1, 2], gbuf.at[1, 3], ym)
    gf_m.start()

    for copy, _, got in halo[8:]:
        pl.when(got)(lambda copy=copy: copy.wait_recv())
    loads[9].wait()
    ge[...] = dot(beside[...], he[:, :, 384:896].reshape(128, 512)).astype(BF16)
    loads[11].wait()

    @pl.loop(0, 12)
    def _(k):
        at = pl.ds(pl.multiple_of(k * 256, 256), 256)
        for n, right in enumerate((gx[...].reshape(256, 512), ge[...])):
            block = dot(wv[at, :], right, ((1,), (1,)))
            pg[2 * n, at, :] = block[:, 0:128]
            pg[2 * n + 1, at, :] = block[:, 128:256]

    q_far_p.wait_recv()
    qf_p = remote(24, rq.at[0], qr.at[3, :, 0:2], yp)
    qf_p.start()
    q_far_m.wait_recv()
    qf_m = remote(25, rq.at[1], qr.at[3, :, 2:4], ym)
    qf_m.start()

    def frames(e, first):
        early = pg[first, pl.ds(e, 192, stride=16), :].reshape(12, 16, 128)
        late = pg[first + 1, pl.ds(e, 192, stride=16), :].reshape(12, 16, 128)
        out = []
        for ch in range(0, 12, 4):
            out += [
                early[ch + 1], early[ch + 2] + late[ch], early[ch + 3] + late[ch + 1], late[ch + 2],
            ]
        return jnp.stack(out)

    j = lax.broadcasted_iota(jnp.int32, (12, 16, 128), 2) % 32
    sub = lax.broadcasted_iota(jnp.int32, (12, 8, 128), 1)
    wrap = {0: (14, 0, 1), 1: (15, 0, 1), 10: (0, 31, 127), 11: (1, 31, 127)}
    for e in range(12):
        cell = frames(e + 2, 0)
        if e in wrap:
            far, at, by = wrap[e]
            cell = cell + jnp.where(j == at, frames(far, 2), pltpu.roll(frames(far, 0), by, 2))
        low, high = cell[:, 0:8], cell[:, 8:16]
        to_low = pltpu.roll(pltpu.roll(high, 32, 2), 4, 1)
        to_high = pltpu.roll(pltpu.roll(low, 96, 2), 4, 1)
        fs[e, :, 0:8] = low + jnp.where((sub == 2) | (sub == 3), to_low, 0.0)
        fs[e, :, 8:16] = high + jnp.where((sub == 4) | (sub == 5), to_high, 0.0)
    block = lax.broadcasted_iota(jnp.int32, (192, 128), 1) // 32
    for i in range(2):
        for k in range(3):
            row = None
            for q in range(4):
                part = fs[4 * k + q].reshape(192, 128)
                by = ((q - i - 1) * 32) % 128
                if by:
                    part = pltpu.roll(part, by, 1)
                row = part if row is None else jnp.where(block == q, part, row)
            upper = row.astype(BF16)
            ll[192 * i : 192 * i + 192, 128 * k : 128 * k + 128] = upper
            ll[384 + 192 * i : 576 + 192 * i, 128 * k : 128 * k + 128] = (row - upper.astype(F32)).astype(BF16)
    loads[10].wait()
    pixels = (dot(ll[0:384, :], back[...]) + dot(ll[384:768, :], back[...])).reshape(2, 12, 16, 384)
    for i in range(2):
        for cf in range(12):
            ch, f = cf // 4, cf % 4
            vg[f // 2, ch * 2 + f % 2, 12 * i : 12 * i + 12, :] = pixels[i, cf, 2:14, :]
    v_x = remote(36, vg.at[1 - m], mr, partner)
    v_x.start()

    for one in (q_p, q_m, qf_p, qf_m, gf_p, gf_m):
        one.wait_recv()
    block = lax.broadcasted_iota(jnp.int32, (64, 128), 1) // 32
    for k in range(4):
        for half in range(2):
            parts = [
                qr[2 * half + n // 2, n % 2, :, :, 128 * k : 128 * k + 128].astype(F32).reshape(64, 128)
                for n in range(4)
            ]
            for q in range(4):
                row = None
                for n in range(4):
                    by = ((n - q) * 32) % 128
                    part = pltpu.roll(parts[n], by, 1) if by else parts[n]
                    row = part if row is None else jnp.where(block == n, part, row)
                lm[0:4, 4 * k + q, :, 128 * half : 128 * half + 128] = row.astype(BF16).reshape(4, 16, 128)
    for ca in range(3):
        total = None
        for t in range(2):
            at = chosen(y, [s[t][ca] for s in SLOTS_OF])
            part = dot(lm[at].reshape(256, 256), gbuf[t].reshape(256, 512))
            total = part if total is None else total + part
        for e in range(16):
            for n in range(4):
                wg[n, pl.ds(ca * 256 + e, 16, stride=16), :] = total[16 * e : 16 * e + 16, 128 * n : 128 * n + 128]

    give = remote(26, wg.at[:, pl.ds((1 - core) * 384, 384)], cr, other)
    give.start()
    give.wait_recv()
    for k in range(16):
        for n in range(4):
            a1[k // 4, k % 4, :, 128 * n : 128 * n + 128] = (
                wg[n, pl.ds(core * 384 + 24 * k, 24), :] + cr[n, 24 * k : 24 * k + 24, :]
            )

    x1, x2, x3 = (x + 1) % 4, (x + 2) % 4, (x + 3) % 4
    far_p = remote(27, a1.at[0:2, x2], xa, xp)
    far_m = remote(28, a1.at[2:4, x2], xb, xm)
    near_p = remote(29, a1.at[2:4, x1], xr1.at[2:4], xp)
    near_m = remote(30, a1.at[0:2, x3], xr2.at[0:2], xm)
    for one in (far_p, far_m, near_p, near_m):
        one.start()
    far_p.wait_recv()
    xs1[...] = a1[0:2, x1] + xa[...]
    last_p = remote(31, xs1, xr1.at[0:2], xp)
    last_p.start()
    far_m.wait_recv()
    xs2[...] = a1[2:4, x3] + xb[...]
    last_m = remote(32, xs2, xr2.at[2:4], xm)
    last_m.start()
    for one in (near_p, near_m, last_p, last_m):
        one.wait_recv()
    a2[...] = a1[:, x] + xr1[...] + xr2[...]

    z_out = [remote(33 + d, a2.at[(z + d + 1) % 4], zr.at[d], zs[d]) for d in (0, 1, 2)]
    for one in z_out:
        one.start()
    v_x.wait_recv()
    vout[...] = vg[m] + mr[...]
    for one in z_out:
        one.wait_recv()
    wout[...] = (a2[z] + zr[0] + (zr[1] + zr[2])) * (1.0 / 128.0)

    for copy, sent, _ in halo:
        pl.when(sent)(lambda copy=copy: copy.wait_send())
    for one in (
        g_p, g_m, gf_p, gf_m, q_far_p, q_far_m, q_p, q_m, qf_p, qf_m, v_x, give,
        far_p, far_m, near_p, near_m, last_p, last_m, *z_out,
    ):
        one.wait_send()


def shards(video, grad_tokens, weight):
    constants = [jnp.asarray(one, BF16) for one in selections()]
    anywhere = pl.BlockSpec(memory_space=pl.ANY)
    in_vmem = pl.BlockSpec(memory_space=pltpu.VMEM)

    def v(*shape, kind=F32):
        return pltpu.VMEM(shape, kind)

    def b(*shape):
        return pltpu.VMEM(shape, BF16)

    video_grad, weight_grad = pl.pallas_call(
        kernel,
        out_shape=(
            jax.ShapeDtypeStruct((6, 24, 384), F32),
            jax.ShapeDtypeStruct((24, 512), F32),
        ),
        in_specs=[anywhere] * 11,
        out_specs=(in_vmem, in_vmem),
        scratch_shapes=[b(*one.shape) for one in constants]
        + [
            b(3072, 512), b(384, 384), b(96, 384), b(8, 16, 896), b(16, 896), b(32, 384),
            b(2, 4, 32, 512), b(256, 512), b(2, 4, 2, 32, 512), b(384, 512), b(12, 2, 16, 512),
            b(3, 2, 4, 16, 512), b(4, 2, 4, 16, 512), b(2, 2, 2, 16, 512), b(5, 16, 16, 256),
            v(4, 3072, 128), v(12, 12, 16, 128), b(768, 384), v(2, 6, 24, 384), v(6, 24, 384),
            v(4, 768, 128), v(4, 384, 128), v(4, 4, 24, 512), v(2, 24, 512), v(2, 24, 512),
            v(4, 24, 512), v(4, 24, 512), v(2, 24, 512), v(2, 24, 512), v(4, 24, 512), v(3, 24, 512),
            pltpu.SemaphoreType.DMA((12,)),
            pltpu.SemaphoreType.DMA((N_SEMS,)),
            pltpu.SemaphoreType.DMA((N_SEMS,)),
        ],
        compiler_params=pltpu.CompilerParams(
            collective_id=0, has_side_effects=True, vmem_limit_bytes=48 * 1024 * 1024
        ),
        name="tubelet_backward",
    )(video.reshape(288, 384), grad_tokens, weight, *constants)
    return video_grad.reshape(3, 2, 24, 384), weight_grad


def solution(mesh):
    return jax.shard_map(
        shards,
        mesh=mesh,
        in_specs=(P(None, None, "row", "col"), P(None, "row", "col", "mp"), P(None, "mp")),
        out_specs=(P(None, "mp", "row", "col"), P(("row", "col"), "mp")),
        check_vma=False,
    )
```

time: 271 us -> 56.5 us (0.21)
  waiting for transfers between devices: 108 us -> 0 us
  local copies, waits for them, and re-layouts: 89.7 us -> 11.7 us
  Pallas kernels: 0 us -> 43.1 us
  other arithmetic: 30 us -> 0 us
  starting transfers between devices: 23.9 us -> 0 us
  between operations: 14 us -> 0.66 us
  matrix products: 4.38 us -> 0 us
    reshape x8 -> x0, local copies, waits for them, and re-layouts: 52.6 us -> none  [the longest x2 16.7 us: unfold_axis(): lower = lower.reshape(shaped)]
    pallas_call x0 -> x1, Pallas kernels: none -> 43.1 us  [shards(): pl.pallas_call(kernel, out_shape=(jax.ShapeDtypeStruct((6, 24, 384), F32)...]
    reduce_scatter x4 -> x0, waiting for transfers between devices: 40 us -> none  [own_block(): parts = lax.psum_scatter(parts, axes[k], scatter_dimension=0, tiled=True)]
    all_to_all x1 -> x0, waiting for transfers between devices: 38.1 us -> none  [summed_on_arrival(): lax.all_to_all(parts, axis, split_axis=0, concat_axis=0, tiled=True)]
    ppermute x9 -> x0, waiting for transfers between devices: 29.5 us -> none  [the longest x4 11.1 us: passed_along(): return lax.ppermute(shard, axis, pairs)]
    ppermute x9 -> x0, starting transfers between devices: 16.8 us -> none  [the longest x4 7.85 us: passed_along(): return lax.ppermute(shard, axis, pairs)]
    transpose x2 -> x0, local copies, waits for them, and re-layouts: 13.1 us -> none  [the longest x1 9.68 us: shards(): patches = pieces.transpose(1, 3, 5, 0, 2, 4, 6).reshape(count, patch)]
    slice x13 -> x0, local copies, waits for them, and re-layouts: 11.5 us -> none  [the longest x2 3.65 us: fold_axis(): lower = lax.slice_in_dim(pieces, 0, stride, axis=axis + 1)]
  transfers between devices with their start and end apart: 14 -> 0, of which waited for: 11 -> 0; matrix products, arithmetic and copies ran while one was open for 17% -> 0% of each run, Pallas kernels for 0% -> 0%
where the time goes in v1:
time: 56.5 us; the launch traced here: 55.5 us
  Pallas kernels  43.1 us (76%)
  local copies, waits for them, and re-layouts  11.7 us (21%)
  between operations  0.66 us (1%)
    pallas_call x1, Pallas kernels, shards(): pl.pallas_call(kernel, out_shape=(jax.ShapeDtypeStruct((6, 24, 384), F32)...  43.1 us
    unnamed x24, local copies, waits for them, and re-layouts  11.7 us

profile of v1, /device:TPU:2, one launch (start us, length us, event | category | flops | bytes accessed | tf_op | source)
XLA Modules:
  0.0 55.5 jit_solution(1778574539635882828)
XLA Ops:
  0.6 0.0 copy-start
  0.6 1.9 %copy-done = bf16[3072,512]{1,0:T(8,128)(2,1)S(1)} copy-done((bf16[3072,512]{1,0:T(8,128)(2,1)S(1)}, bf16[3072,512]{1,0:T(8,128)(2,1)}, u32[]{:S(2)}) %copy-start) | copy-done | bytes 3145752
  2.5 0.0 copy-start.1
  2.5 1.0 %copy-done.1 = bf16[384,512]{1,0:T(8,128)(2,1)S(1)} copy-done((bf16[384,512]{1,0:T(8,128)(2,1)S(1)}, bf16[384,512]{1,0:T(8,128)(2,1)}, u32[]{:S(2)}) %copy-start.1) | copy-done | bytes 393240
  3.5 0.0 copy-start.2
  3.5 1.0 %copy-done.2 = bf16[384,384]{1,0:T(8,128)(2,1)S(1)} copy-done((bf16[384,384]{1,0:T(8,128)(2,1)S(1)}, bf16[384,384]{1,0:T(8,128)(2,1)}, u32[]{:S(2)}) %copy-start.2) | copy-done | bytes 294936
  4.5 0.0 copy-start.3
  4.5 1.0 %copy-done.3 = bf16[384,384]{1,0:T(8,128)(2,1)S(1)} copy-done((bf16[384,384]{1,0:T(8,128)(2,1)S(1)}, bf16[384,384]{1,0:T(8,128)(2,1)}, u32[]{:S(2)}) %copy-start.3) | copy-done | bytes 294936
  5.4 0.0 copy-start.4
  5.4 0.9 %copy-done.4 = bf16[3,4,24,384]{3,2,1,0:T(8,128)(2,1)S(1)} copy-done((bf16[3,4,24,384]{3,2,1,0:T(8,128)(2,1)S(1)}, bf16[3,4,24,384]{3,2,1,0:T(8,128)(2,1)}, u32[]{:S(2)}) %copy-start.4) | copy-done | bytes 221208
  6.4 0.0 copy-start.5
  6.4 0.9 %copy-done.5 = bf16[2,2,32,512]{3,2,1,0:T(8,128)(2,1)S(1)} copy-done((bf16[2,2,32,512]{3,2,1,0:T(8,128)(2,1)S(1)}, bf16[2,2,32,512]{3,2,1,0:T(8,128)(2,1)}, u32[]{:S(2)}) %copy-start.5) | copy-done | bytes 131096
  7.3 0.0 copy-start.6
  7.3 0.8 %copy-done.6 = bf16[256,128]{1,0:T(8,128)(2,1)S(1)} copy-done((bf16[256,128]{1,0:T(8,128)(2,1)S(1)}, bf16[256,128]{1,0:T(8,128)(2,1)}, u32[]{:S(2)}) %copy-start.6) | copy-done | bytes 65560
  8.1 0.0 copy-start.7
  8.1 0.8 %copy-done.7 = bf16[64,288]{1,0:T(8,128)(2,1)S(1)} copy-done((bf16[64,288]{1,0:T(8,128)(2,1)S(1)}, bf16[64,288]{1,0:T(8,128)(2,1)}, u32[]{:S(2)}) %copy-start.7) | copy-done | bytes 36888
  8.9 0.0 copy-start.8
  8.9 0.8 %copy-done.8 = bf16[32,512]{1,0:T(8,128)(2,1)S(1)} copy-done((bf16[32,512]{1,0:T(8,128)(2,1)S(1)}, bf16[32,512]{1,0:T(8,128)(2,1)}, u32[]{:S(2)}) %copy-start.8) | copy-done | bytes 32792
  9.7 0.0 copy-start.9
  9.7 0.7 %copy-done.9 = bf16[16,384]{1,0:T(8,128)(2,1)S(1)} copy-done((bf16[16,384]{1,0:T(8,128)(2,1)S(1)}, bf16[16,384]{1,0:T(8,128)(2,1)}, u32[]{:S(2)}) %copy-start.9) | copy-done | bytes 12312
  10.4 0.0 copy-start.10
  10.4 0.7 %copy-done.10 = bf16[16,128]{1,0:T(8,128)(2,1)S(1)} copy-done((bf16[16,128]{1,0:T(8,128)(2,1)S(1)}, bf16[16,128]{1,0:T(8,128)(2,1)}, u32[]{:S(2)}) %copy-start.10) | copy-done | bytes 4120
  11.1 43.1 %tubelet_backward.1 = (f32[6,24,384]{2,1,0:T(8,128)S(1)}, f32[24,512]{1,0:T(8,128)S(1)}) custom-call(bf16[288,384]{1,0:T(8,128)(2,1)S(1)} %bitcast.3, bf16[2,2,32,512]{3,2,1,0:T(8,128)(2,1)S(1)} %copy-done.5, bf16[3072,512]{1,0:T(8,128)(2,1)S(1)} %copy-done, bf16[384,512]{1,0:T(8,128)(2,1)S(1)} %copy-done.1, bf16[32,512]{1,0:T(8,128)(2,1)S(1)} %copy-done.8, ...), custom_call_target="tpu_custom_call" | custom-call | tf_op jit(solution)/shard_map/tubelet_backward/pallas_call | solution.py:358
  54.2 0.7 %copy.15 = f32[3,2,24,384]{3,2,1,0:T(8,128)} copy(f32[3,2,24,384]{3,2,1,0:T(8,128)S(1)} %bitcast.2) | data formatting | bytes 442368
  54.9 0.6 %copy.16 = f32[24,512]{1,0:T(8,128)} copy(f32[24,512]{1,0:T(8,128)S(1)} %get-tuple-element.9) | data formatting | bytes 98304
Async XLA Ops:
  0.6 1.9 %copy-start = (bf16[3072,512]{1,0:T(8,128)(2,1)S(1)}, bf16[3072,512]{1,0:T(8,128)(2,1)}, u32[]{:S(2)}) copy-start(bf16[3072,512]{1,0:T(8,128)(2,1)} %weight.1) | copy-start | bytes 9437188
  2.5 1.0 %copy-start.1 = (bf16[384,512]{1,0:T(8,128)(2,1)S(1)}, bf16[384,512]{1,0:T(8,128)(2,1)}, u32[]{:S(2)}) copy-start(bf16[384,512]{1,0:T(8,128)(2,1)} %constant.16.clone.cols_h) | copy-start | bytes 1179652
  3.5 1.0 %copy-start.2 = (bf16[384,384]{1,0:T(8,128)(2,1)S(1)}, bf16[384,384]{1,0:T(8,128)(2,1)}, u32[]{:S(2)}) copy-start(bf16[384,384]{1,0:T(8,128)(2,1)} %constant.23.clone.back_h) | copy-start | bytes 884740
  4.5 1.0 %copy-start.3 = (bf16[384,384]{1,0:T(8,128)(2,1)S(1)}, bf16[384,384]{1,0:T(8,128)(2,1)}, u32[]{:S(2)}) copy-start(bf16[384,384]{1,0:T(8,128)(2,1)} %constant.18.clone.rows_h) | copy-start | bytes 884740
  5.4 0.9 %copy-start.4 = (bf16[3,4,24,384]{3,2,1,0:T(8,128)(2,1)S(1)}, bf16[3,4,24,384]{3,2,1,0:T(8,128)(2,1)}, u32[]{:S(2)}) copy-start(bf16[3,4,24,384]{3,2,1,0:T(8,128)(2,1)} %param.11) | copy-start | bytes 663556
  6.4 0.9 %copy-start.5 = (bf16[2,2,32,512]{3,2,1,0:T(8,128)(2,1)S(1)}, bf16[2,2,32,512]{3,2,1,0:T(8,128)(2,1)}, u32[]{:S(2)}) copy-start(bf16[2,2,32,512]{3,2,1,0:T(8,128)(2,1)} %tokens.1) | copy-start | bytes 393220
  7.3 0.8 %copy-start.6 = (bf16[256,128]{1,0:T(8,128)(2,1)S(1)}, bf16[256,128]{1,0:T(8,128)(2,1)}, u32[]{:S(2)}) copy-start(bf16[256,128]{1,0:T(8,128)(2,1)} %constant.22.clone.beside_h) | copy-start | bytes 196612
  8.1 0.8 %copy-start.7 = (bf16[64,288]{1,0:T(8,128)(2,1)S(1)}, bf16[64,288]{1,0:T(8,128)(2,1)}, u32[]{:S(2)}) copy-start(bf16[64,288]{1,0:T(8,128)(2,1)} %constant.20.clone.rim_h) | copy-start | bytes 110596
  8.9 0.8 %copy-start.8 = (bf16[32,512]{1,0:T(8,128)(2,1)S(1)}, bf16[32,512]{1,0:T(8,128)(2,1)}, u32[]{:S(2)}) copy-start(bf16[32,512]{1,0:T(8,128)(2,1)} %constant.17.clone.side_h) | copy-start | bytes 98308
  9.7 0.7 %copy-start.9 = (bf16[16,384]{1,0:T(8,128)(2,1)S(1)}, bf16[16,384]{1,0:T(8,128)(2,1)}, u32[]{:S(2)}) copy-start(bf16[16,384]{1,0:T(8,128)(2,1)} %constant.19.clone.pick_h) | copy-start | bytes 36868
  10.4 0.7 %copy-start.10 = (bf16[16,128]{1,0:T(8,128)(2,1)S(1)}, bf16[16,128]{1,0:T(8,128)(2,1)}, u32[]{:S(2)}) copy-start(bf16[16,128]{1,0:T(8,128)(2,1)} %constant.21.clone.ends_h) | copy-start | bytes 12292

commit v2 on v1

--- a/solution.py
+++ b/solution.py
@@ -376,7 +376,7 @@
             pltpu.SemaphoreType.DMA((N_SEMS,)),
         ],
         compiler_params=pltpu.CompilerParams(
-            collective_id=0, has_side_effects=True, vmem_limit_bytes=48 * 1024 * 1024
+            collective_id=0, has_side_effects=True, vmem_limit_bytes=67043328
         ),
         name="tubelet_backward",
     )(video.reshape(288, 384), grad_tokens, weight, *constants)

time: 56.5 us -> 47.2 us (0.84)
  local copies, waits for them, and re-layouts: 11.7 us -> 3.06 us
    unnamed x24 -> x2, local copies, waits for them, and re-layouts: 11.7 us -> 3.06 us
where the time goes in v2:
time: 47.2 us; the launch traced here: 46.5 us
  Pallas kernels  42.8 us (91%)
  local copies, waits for them, and re-layouts  3.06 us (6%)
  between operations  0.64 us (1%)
    pallas_call x1, Pallas kernels, shards(): pl.pallas_call(kernel, out_shape=(jax.ShapeDtypeStruct((6, 24, 384), F32)...  42.8 us
    unnamed x2, local copies, waits for them, and re-layouts  3.06 us

profile of v2, /device:TPU:2, one launch (start us, length us, event | category | flops | bytes accessed | tf_op | source)
XLA Modules:
  0.0 46.5 jit_solution(11611727593191276034)
XLA Ops:
  0.6 42.8 %tubelet_backward.1 = (f32[6,24,384]{2,1,0:T(8,128)}, f32[24,512]{1,0:T(8,128)}) custom-call(bf16[288,384]{1,0:T(8,128)(2,1)} %bitcast.3, bf16[2,2,32,512]{3,2,1,0:T(8,128)(2,1)} %tokens.1, bf16[3072,512]{1,0:T(8,128)(2,1)} %weight.1, bf16[384,512]{1,0:T(8,128)(2,1)} %constant.16.clone.cols_h, bf16[32,512]{1,0:T(8,128)(2,1)} %constant.17.clone.side_h, ...), custom_call_target="tpu_custom_call" | custom-call | tf_op jit(solution)/shard_map/tubelet_backward/pallas_call | solution.py:358
  43.5 1.6 %copy.15 = f32[3,2,24,384]{3,2,1,0:T(8,128)} copy(f32[3,2,24,384]{3,2,1,0:T(8,128)} %bitcast.2) | data formatting | bytes 442368
  45.1 1.4 %copy.16 = f32[24,512]{1,0:T(8,128)} copy(f32[24,512]{1,0:T(8,128)} %get-tuple-element.9) | data formatting | bytes 98304

commit v3 on v2

v3 whole, which is shorter than its diff:
```python
import jax
import jax.numpy as jnp
import numpy as np
from jax import lax
from jax.experimental import pallas as pl
from jax.experimental.pallas import tpu as pltpu
from jax.sharding import PartitionSpec as P

MESH = pl.DeviceIdType.MESH
F32 = jnp.float32
BF16 = jnp.bfloat16
N_SEMS = 64
VMEM_BYTES = 56500000
PIECES = 2
WIDE = 4 // PIECES
SELECTION_AT = (0, 16, 80, 96, 480, 512, 896, 1152)
SELECTION_ROWS = 1536


def selections():
    cols = np.zeros((384, 512), np.float32)
    for e in range(16):
        for j in range(32):
            x = 12 * j + e - 2
            if 0 <= x < 384:
                cols[x, e * 32 + j] = 1
    side = np.zeros((32, 512), np.float32)
    side[2, 0] = side[3, 32] = 1
    side[16, 14 * 32 + 31] = side[17, 15 * 32 + 31] = 1
    rows = np.zeros((384, 384), np.float32)
    for cf in range(12):
        for i in range(2):
            for b in range(16):
                y = 12 * i + b - 2
                src = cf * 24 + y if 0 <= y < 24 else 288 + cf * 2 + y + 2 if y < 0 else 320 + cf * 2 + y - 24
                rows[cf * 32 + i * 16 + b, src] = 1
    pick = np.zeros((16, 384), np.float32)
    for k, x in enumerate((0, 1, 382, 383)):
        pick[k, x] = 1
    rim = np.zeros((64, 288), np.float32)
    for cf in range(12):
        for k in range(2):
            rim[cf * 2 + k, cf * 24 + 22 + k] = 1
            rim[32 + cf * 2 + k, cf * 24 + k] = 1
    ends = np.zeros((16, 128), np.float32)
    for ti in range(4):
        ends[ti, ti * 32] = 1
        ends[4 + ti, ti * 32 + 31] = 1
    beside = np.zeros((256, 128), np.float32)
    for t in range(2):
        for i4 in range(4):
            i = (1, 0, 1, 0)[i4]
            left = (2, 0, 0, 3)[i4]
            right = (4, 1, 1, 5)[i4]
            beside[t * 128 + i4 * 32, left * 16 + 4 + t * 2 + i] = 1
            beside[t * 128 + i4 * 32 + 31, right * 16 + t * 2 + i] = 1
    back = np.zeros((384, 384), np.float32)
    for e in range(12):
        for j in range(32):
            back[e * 32 + j, 12 * j + e] = 1
    packed = np.zeros((SELECTION_ROWS, 512), np.float32)
    for at, one in zip(SELECTION_AT, (pick, rim, ends, cols, side, rows, beside, back)):
        packed[at : at + one.shape[0], : one.shape[1]] = one
    return packed


def chosen(at, values):
    out = jnp.int32(values[3])
    for k in range(3):
        out = jnp.where(at == k, jnp.int32(values[k]), out)
    return out


FRAMES_OF = ((0, 1, 2, 3), (2, 4, 5, 6), (5, 6, 7, 9), (8, 9, 10, 11))
SLOTS_OF = (
    (((4, 0, 1), (1, 2, 3))),
    (((0, 4, 1), (4, 2, 3))),
    (((0, 1, 4), (2, 4, 3))),
    (((0, 1, 2), (2, 3, 4))),
)


def dot(a, b, dims=((1,), (0,))):
    return lax.dot_general(a, b, (dims, ((), ())), preferred_element_type=F32)


def kernel(
    video, tokens, weight, packed,
    vout, wout,
    sel,
    wv, vs, hv, he, hg, sb, sg, hs, qf, gx, ge, gbuf, qs, qw, sq, qr, rq, lm, pg, fs, ll, vg, mr,
    wg, cr, a1, xa, xb, xr1, xr2, xs1, xs2, a2, zr,
    load, send, recv,
):
    r = lax.axis_index("row")
    c = lax.axis_index("col")
    m = lax.axis_index("mp")
    y, core = r // 2, r % 2
    z, x = c // 4, c % 4

    pairs = [
        (video, vs.at[0:288]), (packed.at[0:96], sel.at[0:96]), (tokens, gx.at[:, 1:3]),
        (tokens, gbuf.at[:, 0]), (packed.at[96:1536], sel.at[96:1536]), (weight, wv),
    ]
    loads = [pltpu.make_async_copy(a, b, load.at[k]) for k, (a, b) in enumerate(pairs)]
    for one in loads:
        one.start()

    pick, rim, ends = sel.at[0:16, 0:384], sel.at[16:80, 0:288], sel.at[80:96, 0:128]
    cols, side, rows = sel.at[96:480], sel.at[480:512], sel.at[512:896, 0:384]
    beside, back = sel.at[896:1152, 0:128], sel.at[1152:1536, 0:384]

    hv[...] = jnp.zeros_like(hv)
    he[...] = jnp.zeros_like(he)
    hg[...] = jnp.zeros_like(hg)
    vs[288:384, :] = jnp.zeros((96, 384), BF16)
    for i4 in (0, 3):
        gx[:, i4] = jnp.zeros((2, 32, 512), BF16)
    lm[4] = jnp.zeros((16, 16, 256), BF16)

    barrier = pltpu.get_barrier_semaphore()
    up, down, lef, rig = r > 0, r < 7, c > 0, c < 15
    near = [
        (up, {"row": r - 1}), (down, {"row": r + 1}), (lef, {"col": c - 1}), (rig, {"col": c + 1}),
        (up & lef, {"row": r - 1, "col": c - 1}), (up & rig, {"row": r - 1, "col": c + 1}),
        (down & lef, {"row": r + 1, "col": c - 1}), (down & rig, {"row": r + 1, "col": c + 1}),
    ]
    yp, ym = {"row": (r + 2) % 8}, {"row": (r + 6) % 8}
    xp, xm = {"col": z * 4 + (x + 1) % 4}, {"col": z * 4 + (x + 3) % 4}
    other = {"row": y * 2 + 1 - core}
    zs = [{"col": ((z + d) % 4) * 4 + x} for d in (1, 2, 3)]
    partner = {"mp": 1 - m}

    def greet(to):
        pl.semaphore_signal(barrier, inc=1, device_id=to, device_id_type=MESH)

    for to in (yp, ym, xp, xm, other, *zs, partner):
        greet(to)
    for there, to in near:
        pl.when(there)(lambda to=to: greet(to))

    def one_if(p):
        return jnp.where(p, jnp.int32(1), jnp.int32(0))

    n_near = (1 + one_if(up) + one_if(down)) * (1 + one_if(lef) + one_if(rig)) - 1

    count = iter(range(N_SEMS))

    def remote(src, dst, to):
        k = next(count)
        return pltpu.make_async_remote_copy(
            src_ref=src, dst_ref=dst, send_sem=send.at[k], recv_sem=recv.at[k],
            device_id=to, device_id_type=MESH,
        )

    for k in range(3):
        loads[k].wait()
    vs[288:352, :] = dot(rim[...], vs[0:288, :]).astype(BF16)
    sb[...] = dot(pick[...], vs[...], ((1,), (1,))).astype(BF16)
    sg[...] = dot(ends[...], gx[:, 1:3].reshape(128, 512)).astype(BF16)
    loads[3].wait()

    pl.semaphore_wait(barrier, 9 + n_near)

    corner = (slice(None), slice(256, 384))
    halo = [
        (remote(vs.at[288:320], hv.at[0:32], {"row": r + 1}), down, up),
        (remote(vs.at[320:352], hv.at[32:64], {"row": r - 1}), up, down),
        (remote(sb, he.at[0], {"col": c + 1}), rig, lef),
        (remote(sb, he.at[1], {"col": c - 1}), lef, rig),
        (remote(sb.at[corner], he.at[2].at[corner], {"row": r + 1, "col": c + 1}), down & rig, up & lef),
        (remote(sb.at[corner], he.at[3].at[corner], {"row": r - 1, "col": c + 1}), up & rig, down & lef),
        (remote(sb.at[corner], he.at[4].at[corner], {"row": r + 1, "col": c - 1}), down & lef, up & rig),
        (remote(sb.at[corner], he.at[5].at[corner], {"row": r - 1, "col": c - 1}), up & lef, down & rig),
    ]
    for copy, sent, _ in halo:
        pl.when(sent)(lambda copy=copy: copy.start())
    g_p = remote(gbuf.at[:, 0], gbuf.at[:, 1], yp)
    g_m = remote(gbuf.at[:, 0], gbuf.at[:, 2], ym)
    g_p.start()
    g_m.start()
    g_in = remote(gx.at[:, 2 - core], gx.at[:, 3 * core], other)
    g_in.start()
    token_halo = [
        (remote(sg, hg.at[0], {"col": c + 1}), rig, lef),
        (remote(sg, hg.at[1], {"col": c - 1}), lef, rig),
        (remote(sg, hg.at[2], {"row": r + 1, "col": c + 1}), down & rig, up & lef),
        (remote(sg, hg.at[3], {"row": r - 1, "col": c + 1}), up & rig, down & lef),
        (remote(sg, hg.at[4], {"row": r + 1, "col": c - 1}), down & lef, up & rig),
        (remote(sg, hg.at[5], {"row": r - 1, "col": c - 1}), up & lef, down & rig),
    ]
    for copy, sent, _ in token_halo:
        pl.when(sent)(lambda copy=copy: copy.start())

    loads[4].wait()
    qf[...] = dot(vs[0:288, :], cols[...])

    for copy, _, got in halo:
        pl.when(got)(lambda copy=copy: copy.wait_recv())

    lane = lax.broadcasted_iota(jnp.int32, (16, 128), 1)
    for k, (a, b, d) in enumerate(((0, 2, 3), (1, 4, 5))):
        hs[16 * k : 16 * k + 16, 0:256] = he[a, :, 0:256]
        tile = jnp.where(
            lane < 32, he[a, :, 256:384].astype(F32),
            jnp.where(lane < 64, he[b, :, 256:384].astype(F32), he[d, :, 256:384].astype(F32)),
        )
        hs[16 * k : 16 * k + 16, 256:384] = tile.astype(BF16)
    from_side = dot(hs[...], side[...], ((0,), (0,)))
    qs[0:288, :] = (qf[...] + from_side[0:288]).astype(BF16)
    qs[288:384, :] = (dot(hv[...], cols[...]) + from_side[288:384]).astype(BF16)
    qw[...] = dot(rows[...], qs[...]).astype(BF16).reshape(12, 2, 16, 512)

    for d, to in ((2, 2), (0, 1), (1, 3)):
        for s in range(4):
            at = chosen((y + to) % 4, [f[s] for f in FRAMES_OF])
            sq[d, :, s] = qw[at]
    q_far_p = remote(sq.at[2, :, 0:2], rq.at[0], yp)
    q_far_m = remote(sq.at[2, :, 2:4], rq.at[1], ym)
    q_p = remote(sq.at[0], qr.at[1], yp)
    q_m = remote(sq.at[1], qr.at[2], ym)
    for one in (q_far_p, q_far_m, q_p, q_m):
        one.start()
    for s in range(4):
        at = chosen(y, [f[s] for f in FRAMES_OF])
        qr[0, :, s] = qw[at]

    g_p.wait_recv()
    gf_p = remote(gbuf.at[0, 1], gbuf.at[0, 3], yp)
    gf_p.start()
    g_m.wait_recv()
    gf_m = remote(gbuf.at[1, 2], gbuf.at[1, 3], ym)
    gf_m.start()
    g_out = remote(gbuf.at[:, 2 - core, core], gx.at[:, 3 - 3 * core], other)
    g_sent = ((core == 0) & (y < 3)) | ((core == 1) & (y > 0))
    g_got = ((core == 0) & (y > 0)) | ((core == 1) & (y < 3))
    pl.when(g_sent)(g_out.start)

    g_in.wait_recv()
    pl.when(g_got)(g_out.wait_recv)
    for copy, _, got in token_halo:
        pl.when(got)(lambda copy=copy: copy.wait_recv())
    loads[5].wait()

    ge[...] = dot(beside[...], hg[...].reshape(128, 512)).astype(BF16)

    def token_grads(first, last):
        @pl.loop(first, last)
        def _(k):
            at = pl.ds(pl.multiple_of(k * 256, 256), 256)
            for n, right in enumerate((gx[...].reshape(256, 512), ge[...])):
                block = dot(wv[at, :], right, ((1,), (1,)))
                pg[2 * n, at, :] = block[:, 0:128]
                pg[2 * n + 1, at, :] = block[:, 128:256]

    token_grads(0, 6)

    q_far_p.wait_recv()
    qf_p = remote(rq.at[0], qr.at[3, :, 0:2], yp)
    qf_p.start()
    q_far_m.wait_recv()
    qf_m = remote(rq.at[1], qr.at[3, :, 2:4], ym)
    qf_m.start()

    token_grads(6, 12)

    def frames(e, first):
        early = pg[first, pl.ds(e, 192, stride=16), :].reshape(12, 16, 128)
        late = pg[first + 1, pl.ds(e, 192, stride=16), :].reshape(12, 16, 128)
        out = []
        for ch in range(0, 12, 4):
            out += [
                early[ch + 1], early[ch + 2] + late[ch], early[ch + 3] + late[ch + 1], late[ch + 2],
            ]
        return jnp.stack(out)

    j = lax.broadcasted_iota(jnp.int32, (12, 16, 128), 2) % 32
    sub = lax.broadcasted_iota(jnp.int32, (12, 8, 128), 1)
    wrap = {0: (14, 0, 1), 1: (15, 0, 1), 10: (0, 31, 127), 11: (1, 31, 127)}
    for e in range(12):
        cell = frames(e + 2, 0)
        if e in wrap:
            far, at, by = wrap[e]
            cell = cell + jnp.where(j == at, frames(far, 2), pltpu.roll(frames(far, 0), by, 2))
        low, high = cell[:, 0:8], cell[:, 8:16]
        to_low = pltpu.roll(pltpu.roll(high, 32, 2), 4, 1)
        to_high = pltpu.roll(pltpu.roll(low, 96, 2), 4, 1)
        fs[e, :, 0:8] = low + jnp.where((sub == 2) | (sub == 3), to_low, 0.0)
        fs[e, :, 8:16] = high + jnp.where((sub == 4) | (sub == 5), to_high, 0.0)
    block = lax.broadcasted_iota(jnp.int32, (192, 128), 1) // 32
    for i in range(2):
        for k in range(3):
            row = None
            for q in range(4):
                part = fs[4 * k + q].reshape(192, 128)
                by = ((q - i - 1) * 32) % 128
                if by:
                    part = pltpu.roll(part, by, 1)
                row = part if row is None else jnp.where(block == q, part, row)
            upper = row.astype(BF16)
            ll[192 * i : 192 * i + 192, 128 * k : 128 * k + 128] = upper
            ll[384 + 192 * i : 576 + 192 * i, 128 * k : 128 * k + 128] = (row - upper.astype(F32)).astype(BF16)
    pixels = (dot(ll[0:384, :], back[...]) + dot(ll[384:768, :], back[...])).reshape(2, 12, 16, 384)
    for i in range(2):
        for cf in range(12):
            ch, f = cf // 4, cf % 4
            vg[f // 2, ch * 2 + f % 2, 12 * i : 12 * i + 12, :] = pixels[i, cf, 2:14, :]
    v_x = remote(vg.at[1 - m], mr, partner)
    v_x.start()

    for one in (q_p, q_m, qf_p, qf_m, gf_p, gf_m):
        one.wait_recv()

    block = lax.broadcasted_iota(jnp.int32, (64, 128), 1) // 32
    for k in range(4):
        for half in range(2):
            parts = [
                qr[2 * half + n // 2, n % 2, :, :, 128 * k : 128 * k + 128].astype(F32).reshape(64, 128)
                for n in range(4)
            ]
            for q in range(4):
                row = None
                for n in range(4):
                    by = ((n - q) * 32) % 128
                    part = pltpu.roll(parts[n], by, 1) if by else parts[n]
                    row = part if row is None else jnp.where(block == n, part, row)
                lm[0:4, 4 * k + q, :, 128 * half : 128 * half + 128] = row.astype(BF16).reshape(4, 16, 128)

    give = []
    for p in range(PIECES):
        for ca in range(3):
            total = None
            for t in range(2):
                at = chosen(y, [s[t][ca] for s in SLOTS_OF])
                right = gbuf[t, :, :, :, 128 * WIDE * p : 128 * WIDE * (p + 1)].reshape(256, 128 * WIDE)
                part = dot(lm[at].reshape(256, 256), right)
                total = part if total is None else total + part
            for e in range(16):
                for n in range(WIDE):
                    wg[WIDE * p + n, pl.ds(ca * 256 + e, 16, stride=16), :] = (
                        total[16 * e : 16 * e + 16, 128 * n : 128 * n + 128]
                    )
        tiles = slice(WIDE * p, WIDE * p + WIDE)
        give.append(remote(wg.at[tiles, pl.ds((1 - core) * 384, 384)], cr.at[tiles], other))
        give[p].start()

    x1, x2, x3 = (x + 1) % 4, (x + 2) % 4, (x + 3) % 4
    far_p, far_m, near_p, near_m, last_p, last_m = [], [], [], [], [], []
    for p in range(PIECES):
        tiles = slice(WIDE * p, WIDE * p + WIDE)
        give[p].wait_recv()
        for n in range(WIDE * p, WIDE * p + WIDE):
            for k in range(16):
                a1[n, k // 4, k % 4] = wg[n, pl.ds(core * 384 + 24 * k, 24), :] + cr[n, 24 * k : 24 * k + 24, :]
        far_p.append(remote(a1.at[tiles, 0:2, x2], xa.at[tiles], xp))
        far_m.append(remote(a1.at[tiles, 2:4, x2], xb.at[tiles], xm))
        far_p[p].start()
        far_m[p].start()
    for p in range(PIECES):
        tiles = slice(WIDE * p, WIDE * p + WIDE)
        near_p.append(remote(a1.at[tiles, 2:4, x1], xr1.at[tiles, 2:4], xp))
        near_m.append(remote(a1.at[tiles, 0:2, x3], xr2.at[tiles, 0:2], xm))
        near_p[p].start()
        near_m[p].start()

    for p in range(PIECES):
        tiles = slice(WIDE * p, WIDE * p + WIDE)
        far_p[p].wait_recv()
        xs1[tiles] = a1[tiles, 0:2, x1] + xa[tiles]
        last_p.append(remote(xs1.at[tiles], xr1.at[tiles, 0:2], xp))
        last_p[p].start()
        far_m[p].wait_recv()
        xs2[tiles] = a1[tiles, 2:4, x3] + xb[tiles]
        last_m.append(remote(xs2.at[tiles], xr2.at[tiles, 2:4], xm))
        last_m[p].start()

    z_out = []
    for p in range(PIECES):
        tiles = slice(WIDE * p, WIDE * p + WIDE)
        for one in (near_p, near_m, last_p, last_m):
            one[p].wait_recv()
        a2[tiles] = a1[tiles, :, x] + xr1[tiles] + xr2[tiles]
        z_out.append([remote(a2.at[tiles, (z + d + 1) % 4], zr.at[d, tiles], zs[d]) for d in (2, 1, 0)])
        for one in z_out[p]:
            one.start()

    v_x.wait_recv()
    vg[m] = vg[m] + mr[...]
    v_out = pltpu.make_async_copy(vg.at[m], vout, load.at[6])
    v_out.start()

    for p in range(PIECES):
        for one in z_out[p]:
            one.wait_recv()
        for n in range(WIDE * p, WIDE * p + WIDE):
            wout[:, 128 * n : 128 * n + 128] = (a2[n, z] + zr[0, n] + (zr[1, n] + zr[2, n])) * (1.0 / 128.0)

    v_out.wait()
    for copy, sent, _ in halo + token_halo:
        pl.when(sent)(lambda copy=copy: copy.wait_send())
    pl.when(g_sent)(g_out.wait_send)
    for one in (
        g_p, g_m, g_in, gf_p, gf_m, q_far_p, q_far_m, q_p, q_m, qf_p, qf_m, v_x,
        *give, *far_p, *far_m, *near_p, *near_m, *last_p, *last_m, *sum(z_out, []),
    ):
        one.wait_send()


def shards(video, grad_tokens, weight):
    packed = jnp.asarray(selections(), BF16)
    anywhere = pl.BlockSpec(memory_space=pltpu.HBM)
    in_vmem = pl.BlockSpec(memory_space=pltpu.VMEM)

    def v(*shape, kind=F32):
        return pltpu.VMEM(shape, kind)

    def b(*shape):
        return pltpu.VMEM(shape, BF16)

    video_grad, weight_grad = pl.pallas_call(
        kernel,
        out_shape=(
            jax.ShapeDtypeStruct((6, 24, 384), F32),
            jax.ShapeDtypeStruct((24, 512), F32),
        ),
        in_specs=[anywhere] * 4,
        out_specs=(pl.BlockSpec(memory_space=pl.ANY), in_vmem),
        scratch_shapes=[
            b(SELECTION_ROWS, 512),
            b(3072, 512), b(384, 384), b(96, 384), b(6, 16, 384), b(8, 16, 512), b(16, 384), b(16, 512), b(32, 384), v(288, 512),
            b(2, 4, 32, 512), b(256, 512), b(2, 4, 2, 32, 512), b(384, 512), b(12, 2, 16, 512),
            b(3, 2, 4, 16, 512), b(4, 2, 4, 16, 512), b(2, 2, 2, 16, 512), b(5, 16, 16, 256),
            v(4, 3072, 128), v(12, 12, 16, 128), b(768, 384), v(2, 6, 24, 384), v(6, 24, 384),
            v(4, 768, 128), v(4, 384, 128), v(4, 4, 4, 24, 128), v(4, 2, 24, 128), v(4, 2, 24, 128),
            v(4, 4, 24, 128), v(4, 4, 24, 128), v(4, 2, 24, 128), v(4, 2, 24, 128), v(4, 4, 24, 128),
            v(3, 4, 24, 128),
            pltpu.SemaphoreType.DMA((7,)),
            pltpu.SemaphoreType.DMA((N_SEMS,)),
            pltpu.SemaphoreType.DMA((N_SEMS,)),
        ],
        compiler_params=pltpu.CompilerParams(
            collective_id=0, has_side_effects=True, vmem_limit_bytes=VMEM_BYTES
        ),
        name="tubelet_backward",
    )(video.reshape(288, 384), grad_tokens, weight, packed)
    return video_grad.reshape(3, 2, 24, 384), weight_grad


def solution(mesh):
    return jax.shard_map(
        shards,
        mesh=mesh,
        in_specs=(P(None, None, "row", "col"), P(None, "row", "col", "mp"), P(None, "mp")),
        out_specs=(P(None, "mp", "row", "col"), P(("row", "col"), "mp")),
        check_vma=False,
    )
```

time: 47.2 us -> 45.3 us (0.960)
  the two profiles are of different devices: /device:TPU:2 before, /device:TPU:1 now
where the time goes in v3:
time: 45.3 us; the launch traced here: 45.2 us
  Pallas kernels  42.3 us (93%)
  local copies, waits for them, and re-layouts  2.26 us (5%)
  between operations  0.64 us (1%)
    pallas_call x1, Pallas kernels, shards(): pl.pallas_call(kernel, out_shape=(jax.ShapeDtypeStruct((6, 24, 384), F32)...  42.3 us
    unnamed x2, local copies, waits for them, and re-layouts  2.26 us

profile of v3, /device:TPU:1, one launch (start us, length us, event | category | flops | bytes accessed | tf_op | source)
XLA Modules:
  0.0 45.2 jit_solution(5258822207770039845)
XLA Ops:
  0.6 42.3 %tubelet_backward.1 = (f32[6,24,384]{2,1,0:T(8,128)}, f32[24,512]{1,0:T(8,128)S(1)}) custom-call(bf16[288,384]{1,0:T(8,128)(2,1)} %bitcast.3, bf16[2,2,32,512]{3,2,1,0:T(8,128)(2,1)} %tokens.1, bf16[3072,512]{1,0:T(8,128)(2,1)} %weight.1, bf16[1536,512]{1,0:T(8,128)(2,1)} %constant.2.clone.packed), custom_call_target="tpu_custom_call" | custom-call | tf_op jit(solution)/shard_map/tubelet_backward/pallas_call | solution.py:420
  43.0 1.6 %copy.8 = f32[3,2,24,384]{3,2,1,0:T(8,128)} copy(f32[3,2,24,384]{3,2,1,0:T(8,128)} %bitcast.2) | data formatting | bytes 442368
  44.6 0.6 %copy.9 = f32[24,512]{1,0:T(8,128)} copy(f32[24,512]{1,0:T(8,128)S(1)} %get-tuple-element.9) | data formatting | bytes 98304

commit v4 on v3

--- a/solution.py
+++ b/solution.py
@@ -13,6 +13,7 @@
 VMEM_BYTES = 56500000
 PIECES = 2
 WIDE = 4 // PIECES
+CODED = WIDE * 48
 SELECTION_AT = (0, 16, 80, 96, 480, 512, 896, 1152)
 SELECTION_ROWS = 1536
 
@@ -84,12 +85,42 @@
     return lax.dot_general(a, b, (dims, ((), ())), preferred_element_type=F32)
 
 
+TOP = 2.0**15
+
+
+def largest(x):
+    top = jnp.abs(x).reshape(-1, x.shape[-1])
+    top = jnp.max(jnp.max(top, axis=0, keepdims=True), axis=1, keepdims=True)
+    return (jnp.maximum(top, 1e-25) * 1.01).astype(BF16).astype(F32)
+
+
+def packed_rows(x):
+    return x.reshape(-1, x.shape[-1])
+
+
+def coded(x, top):
+    t = packed_rows(x) * (TOP / top)
+    t2 = t * t
+    t4 = t2 * t2
+    return (t4 * t2 * jnp.abs(t) * t).astype(BF16)
+
+
+def decoded(code, top, shape):
+    v = code.astype(F32)
+    t = jnp.sqrt(jnp.sqrt(jnp.sqrt(jnp.abs(v)))) * (top * (1.0 / TOP))
+    return jnp.where(v < 0, -t, t).reshape(shape)
+
+
+def spread(top, lanes):
+    return jnp.broadcast_to(top, (16, lanes)).astype(BF16)
+
+
 def kernel(
     video, tokens, weight, packed,
     vout, wout,
     sel,
-    wv, vs, hv, he, hg, sb, sg, hs, qf, gx, ge, gbuf, qs, qw, sq, qr, rq, lm, pg, fs, ll, vg, mr,
-    wg, cr, a1, xa, xb, xr1, xr2, xs1, xs2, a2, zr,
+    wv, vs, hv, he, hg, sb, sg, hs, qf, gx, ge, gbuf, qs, qw, sq, qr, rq, lm, pg, fs, ll, vg, ms, mr,
+    wg, cr, a1, fo, fi, no, ni, lo, li, a2, zr,
     load, send, recv,
 ):
     r = lax.axis_index("row")
@@ -305,7 +336,10 @@
         for cf in range(12):
             ch, f = cf // 4, cf % 4
             vg[f // 2, ch * 2 + f % 2, 12 * i : 12 * i + 12, :] = pixels[i, cf, 2:14, :]
-    v_x = remote(vg.at[1 - m], mr, partner)
+    top = largest(vg[1 - m])
+    ms[0:16] = spread(top, 384)
+    ms[16:160] = coded(vg[1 - m], top)
+    v_x = remote(ms, mr, partner)
     v_x.start()
 
     for one in (q_p, q_m, qf_p, qf_m, gf_p, gf_m):
@@ -345,47 +379,59 @@
         give[p].start()
 
     x1, x2, x3 = (x + 1) % 4, (x + 2) % 4, (x + 3) % 4
-    far_p, far_m, near_p, near_m, last_p, last_m = [], [], [], [], [], []
+    far, near, last, tops = [], [], [], []
+    halves = (slice(0, 2), slice(2, 4))
+    ring = (xp, xm)
+    beyond = (x1, x3)
+    block = (WIDE, 2, 24, 128)
     for p in range(PIECES):
         tiles = slice(WIDE * p, WIDE * p + WIDE)
         give[p].wait_recv()
         for n in range(WIDE * p, WIDE * p + WIDE):
             for k in range(16):
                 a1[n, k // 4, k % 4] = wg[n, pl.ds(core * 384 + 24 * k, 24), :] + cr[n, 24 * k : 24 * k + 24, :]
-        far_p.append(remote(a1.at[tiles, 0:2, x2], xa.at[tiles], xp))
-        far_m.append(remote(a1.at[tiles, 2:4, x2], xb.at[tiles], xm))
-        far_p[p].start()
-        far_m[p].start()
+        tops.append(largest(a1[tiles]))
+        for d in range(2):
+            fo[d, p, 0:16] = spread(tops[p], 128)
+            fo[d, p, 16:] = coded(a1[tiles, halves[d], x2], tops[p])
+            far.append(remote(fo.at[d, p], fi.at[d, p], ring[d]))
+            far[-1].start()
     for p in range(PIECES):
         tiles = slice(WIDE * p, WIDE * p + WIDE)
-        near_p.append(remote(a1.at[tiles, 2:4, x1], xr1.at[tiles, 2:4], xp))
-        near_m.append(remote(a1.at[tiles, 0:2, x3], xr2.at[tiles, 0:2], xm))
-        near_p[p].start()
-        near_m[p].start()
+        for d in range(2):
+            no[d, p] = coded(a1[tiles, halves[1 - d], beyond[d]], tops[p])
+            near.append(remote(no.at[d, p], ni.at[d, p], ring[d]))
+            near[-1].start()
 
     for p in range(PIECES):
         tiles = slice(WIDE * p, WIDE * p + WIDE)
-        far_p[p].wait_recv()
-        xs1[tiles] = a1[tiles, 0:2, x1] + xa[tiles]
-        last_p.append(remote(xs1.at[tiles], xr1.at[tiles, 0:2], xp))
-        last_p[p].start()
-        far_m[p].wait_recv()
-        xs2[tiles] = a1[tiles, 2:4, x3] + xb[tiles]
-        last_m.append(remote(xs2.at[tiles], xr2.at[tiles, 2:4], xm))
-        last_m[p].start()
+        for d in range(2):
+            far[2 * p + d].wait_recv()
+            top = fi[d, p, 0:16].astype(F32)[0:1]
+            total = a1[tiles, halves[d], beyond[d]] + decoded(fi[d, p, 16:], top, block)
+            top = ((top[:, 0:1] + tops[p]) * 1.01).astype(BF16).astype(F32)
+            lo[d, p, 0:16] = spread(top, 128)
+            lo[d, p, 16:] = coded(total, top)
+            last.append(remote(lo.at[d, p], li.at[d, p], ring[d]))
+            last[-1].start()
 
     z_out = []
     for p in range(PIECES):
         tiles = slice(WIDE * p, WIDE * p + WIDE)
-        for one in (near_p, near_m, last_p, last_m):
-            one[p].wait_recv()
-        a2[tiles] = a1[tiles, :, x] + xr1[tiles] + xr2[tiles]
+        for d in range(2):
+            near[2 * p + d].wait_recv()
+            top = fi[d, p, 0:16].astype(F32)[0:1]
+            a1[tiles, halves[1 - d], x] = a1[tiles, halves[1 - d], x] + decoded(ni[d, p], top, block)
+        for d in range(2):
+            last[2 * p + d].wait_recv()
+            top = li[d, p, 0:16].astype(F32)[0:1]
+            a2[tiles, halves[d]] = a1[tiles, halves[d], x] + decoded(li[d, p, 16:], top, block)
         z_out.append([remote(a2.at[tiles, (z + d + 1) % 4], zr.at[d, tiles], zs[d]) for d in (2, 1, 0)])
         for one in z_out[p]:
             one.start()
 
     v_x.wait_recv()
-    vg[m] = vg[m] + mr[...]
+    vg[m] = vg[m] + decoded(mr[16:160], mr[0:16].astype(F32)[0:1], (6, 24, 384))
     v_out = pltpu.make_async_copy(vg.at[m], vout, load.at[6])
     v_out.start()
 
@@ -401,7 +447,7 @@
     pl.when(g_sent)(g_out.wait_send)
     for one in (
         g_p, g_m, g_in, gf_p, gf_m, q_far_p, q_far_m, q_p, q_m, qf_p, qf_m, v_x,
-        *give, *far_p, *far_m, *near_p, *near_m, *last_p, *last_m, *sum(z_out, []),
+        *give, *far, *near, *last, *sum(z_out, []),
     ):
         one.wait_send()
 
@@ -430,9 +476,10 @@
             b(3072, 512), b(384, 384), b(96, 384), b(6, 16, 384), b(8, 16, 512), b(16, 384), b(16, 512), b(32, 384), v(288, 512),
             b(2, 4, 32, 512), b(256, 512), b(2, 4, 2, 32, 512), b(384, 512), b(12, 2, 16, 512),
             b(3, 2, 4, 16, 512), b(4, 2, 4, 16, 512), b(2, 2, 2, 16, 512), b(5, 16, 16, 256),
-            v(4, 3072, 128), v(12, 12, 16, 128), b(768, 384), v(2, 6, 24, 384), v(6, 24, 384),
-            v(4, 768, 128), v(4, 384, 128), v(4, 4, 4, 24, 128), v(4, 2, 24, 128), v(4, 2, 24, 128),
-            v(4, 4, 24, 128), v(4, 4, 24, 128), v(4, 2, 24, 128), v(4, 2, 24, 128), v(4, 4, 24, 128),
+            v(4, 3072, 128), v(12, 12, 16, 128), b(768, 384), v(2, 6, 24, 384), b(160, 384), b(160, 384),
+            v(4, 768, 128), v(4, 384, 128), v(4, 4, 4, 24, 128),
+            *[b(2, PIECES, rows, 128) for rows in (CODED + 16, CODED + 16, CODED, CODED, CODED + 16, CODED + 16)],
+            v(4, 4, 24, 128),
             v(3, 4, 24, 128),
             pltpu.SemaphoreType.DMA((7,)),
             pltpu.SemaphoreType.DMA((N_SEMS,)),

time: 45.3 us -> 43.2 us (0.954)
  Pallas kernels: 42.3 us -> 40.2 us
    pallas_call x1, Pallas kernels: 42.3 us -> 40.2 us  [shards(): pl.pallas_call(kernel, out_shape=(jax.ShapeDtypeStruct((6, 24, 384), F32)...]
where the time goes in v4:
time: 43.2 us; the launch traced here: 43.1 us
  Pallas kernels  40.2 us (93%)
  local copies, waits for them, and re-layouts  2.26 us (5%)
  between operations  0.64 us (1%)
    pallas_call x1, Pallas kernels, shards(): pl.pallas_call(kernel, out_shape=(jax.ShapeDtypeStruct((6, 24, 384), F32)...  40.2 us
    unnamed x2, local copies, waits for them, and re-layouts  2.26 us

profile of v4, /device:TPU:1, one launch (start us, length us, event | category | flops | bytes accessed | tf_op | source)
XLA Modules:
  0.0 43.1 jit_solution(5796589429671511288)
XLA Ops:
  0.6 40.2 %tubelet_backward.1 = (f32[6,24,384]{2,1,0:T(8,128)}, f32[24,512]{1,0:T(8,128)S(1)}) custom-call(bf16[288,384]{1,0:T(8,128)(2,1)} %bitcast.3, bf16[2,2,32,512]{3,2,1,0:T(8,128)(2,1)} %tokens.1, bf16[3072,512]{1,0:T(8,128)(2,1)} %weight.1, bf16[1536,512]{1,0:T(8,128)(2,1)} %constant.2.clone.packed), custom_call_target="tpu_custom_call" | custom-call | tf_op jit(solution)/shard_map/tubelet_backward/pallas_call | solution.py:466
  40.9 1.6 %copy.8 = f32[3,2,24,384]{3,2,1,0:T(8,128)} copy(f32[3,2,24,384]{3,2,1,0:T(8,128)} %bitcast.2) | data formatting | bytes 442368
  42.5 0.6 %copy.9 = f32[24,512]{1,0:T(8,128)} copy(f32[24,512]{1,0:T(8,128)S(1)} %get-tuple-element.9) | data formatting | bytes 98304

commit v5 on v4

--- a/solution.py
+++ b/solution.py
@@ -9,13 +9,14 @@
 MESH = pl.DeviceIdType.MESH
 F32 = jnp.float32
 BF16 = jnp.bfloat16
-N_SEMS = 64
+N_SEMS = 80
+FRAMES_OF = ((0, 1, 2, 3), (2, 4, 5, 6), (5, 6, 7, 9), (8, 9, 10, 11))
 VMEM_BYTES = 56500000
 PIECES = 2
 WIDE = 4 // PIECES
 CODED = WIDE * 48
-SELECTION_AT = (0, 16, 80, 96, 480, 512, 896, 1152)
-SELECTION_ROWS = 1536
+SELECTION_AT = (0, 16, 80, 96, 480, 496, 880, 1008, 1136, 1200, 1456)
+SELECTION_ROWS = 1840
 
 
 def selections():
@@ -25,16 +26,29 @@
             x = 12 * j + e - 2
             if 0 <= x < 384:
                 cols[x, e * 32 + j] = 1
-    side = np.zeros((32, 512), np.float32)
+    side = np.zeros((16, 512), np.float32)
     side[2, 0] = side[3, 32] = 1
-    side[16, 14 * 32 + 31] = side[17, 15 * 32 + 31] = 1
-    rows = np.zeros((384, 384), np.float32)
-    for cf in range(12):
-        for i in range(2):
+    side[0, 14 * 32 + 31] = side[1, 15 * 32 + 31] = 1
+    rim_of = np.zeros((64, 64), np.float32)
+    places = np.zeros((384, 512), np.float32)
+    for at in range(4):
+        for s, cf in enumerate(FRAMES_OF[at]):
+            for k in range(24):
+                places[cf * 24 + k, at * 128 + s * 32 + k] = 1
+            for k in range(4):
+                far = (k // 2) * 32 + cf * 2 + k % 2
+                rim_of[at * 16 + s * 4 + k, far] = 1
+                places[288 + far, at * 128 + s * 32 + 24 + k] = 1
+    rows = np.zeros((128, 128), np.float32)
+    rows_far = np.zeros((128, 16), np.float32)
+    for i in range(2):
+        for s in range(4):
             for b in range(16):
                 y = 12 * i + b - 2
-                src = cf * 24 + y if 0 <= y < 24 else 288 + cf * 2 + y + 2 if y < 0 else 320 + cf * 2 + y - 24
-                rows[cf * 32 + i * 16 + b, src] = 1
+                k = y + 2 if y < 0 else y - 22
+                rows[i * 64 + s * 16 + b, s * 32 + (y if 0 <= y < 24 else 24 + k)] = 1
+                if not 0 <= y < 24:
+                    rows_far[i * 64 + s * 16 + b, s * 4 + k] = 1
     pick = np.zeros((16, 384), np.float32)
     for k, x in enumerate((0, 1, 382, 383)):
         pick[k, x] = 1
@@ -60,7 +74,7 @@
         for j in range(32):
             back[e * 32 + j, 12 * j + e] = 1
     packed = np.zeros((SELECTION_ROWS, 512), np.float32)
-    for at, one in zip(SELECTION_AT, (pick, rim, ends, cols, side, rows, beside, back)):
+    for at, one in zip(SELECTION_AT, (pick, rim, ends, cols, side, places, rows, rows_far, rim_of, beside, back)):
         packed[at : at + one.shape[0], : one.shape[1]] = one
     return packed
 
@@ -72,7 +86,6 @@
     return out
 
 
-FRAMES_OF = ((0, 1, 2, 3), (2, 4, 5, 6), (5, 6, 7, 9), (8, 9, 10, 11))
 SLOTS_OF = (
     (((4, 0, 1), (1, 2, 3))),
     (((0, 4, 1), (4, 2, 3))),
@@ -116,10 +129,10 @@
 
 
 def kernel(
-    video, tokens, weight, packed,
+    video, frames_h, tokens, weight, packed,
     vout, wout,
     sel,
-    wv, vs, hv, he, hg, sb, sg, hs, qf, gx, ge, gbuf, qs, qw, sq, qr, rq, lm, pg, fs, ll, vg, ms, mr,
+    wv, vs, v3, rv, rq, hv, he, hg, sb, sg, hs, ex, er, gx, ge, gbuf, qr, lm, pg, fs, ll, vg, ms, mr,
     wg, cr, a1, fo, fi, no, ni, lo, li, a2, zr,
     load, send, recv,
 ):
@@ -131,15 +144,19 @@
 
     pairs = [
         (video, vs.at[0:288]), (packed.at[0:96], sel.at[0:96]), (tokens, gx.at[:, 1:3]),
-        (tokens, gbuf.at[:, 0]), (packed.at[96:1536], sel.at[96:1536]), (weight, wv),
+        (tokens, gbuf.at[:, 0]), (frames_h, v3), (packed.at[96:SELECTION_ROWS], sel.at[96:SELECTION_ROWS]),
+        (weight, wv),
     ]
+    for s in range(4):
+        pairs.append((frames_h.at[chosen(y, [f[s] for f in FRAMES_OF])], rv.at[0, s, 0:24]))
     loads = [pltpu.make_async_copy(a, b, load.at[k]) for k, (a, b) in enumerate(pairs)]
     for one in loads:
         one.start()
 
     pick, rim, ends = sel.at[0:16, 0:384], sel.at[16:80, 0:288], sel.at[80:96, 0:128]
-    cols, side, rows = sel.at[96:480], sel.at[480:512], sel.at[512:896, 0:384]
-    beside, back = sel.at[896:1152, 0:128], sel.at[1152:1536, 0:384]
+    cols, side, places = sel.at[96:480], sel.at[480:496], sel.at[496:880]
+    rows, rows_far, rim_of = sel.at[880:1008, 0:128], sel.at[1008:1136, 0:16], sel.at[1136:1200, 0:64]
+    beside, back = sel.at[1200:1456, 0:128], sel.at[1456:1840, 0:384]
 
     hv[...] = jnp.zeros_like(hv)
     he[...] = jnp.zeros_like(he)
@@ -147,6 +164,7 @@
     vs[288:384, :] = jnp.zeros((96, 384), BF16)
     for i4 in (0, 3):
         gx[:, i4] = jnp.zeros((2, 32, 512), BF16)
+    rv[:, :, 24:32] = jnp.zeros((4, 4, 8, 384), BF16)
     lm[4] = jnp.zeros((16, 16, 256), BF16)
 
     barrier = pltpu.get_barrier_semaphore()
@@ -165,7 +183,7 @@
     def greet(to):
         pl.semaphore_signal(barrier, inc=1, device_id=to, device_id_type=MESH)
 
-    for to in (yp, ym, xp, xm, other, *zs, partner):
+    for to in (yp, ym, {"row": (r + 4) % 8}, xp, xm, other, *zs, partner):
         greet(to)
     for there, to in near:
         pl.when(there)(lambda to=to: greet(to))
@@ -190,8 +208,9 @@
     sb[...] = dot(pick[...], vs[...], ((1,), (1,))).astype(BF16)
     sg[...] = dot(ends[...], gx[:, 1:3].reshape(128, 512)).astype(BF16)
     loads[3].wait()
-
-    pl.semaphore_wait(barrier, 9 + n_near)
+    loads[4].wait()
+
+    pl.semaphore_wait(barrier, 10 + n_near)
 
     corner = (slice(None), slice(256, 384))
     halo = [
@@ -206,10 +225,18 @@
     ]
     for copy, sent, _ in halo:
         pl.when(sent)(lambda copy=copy: copy.start())
+
+    def slice_of(to, s):
+        return v3.at[chosen((y + to) % 4, [f[s] for f in FRAMES_OF])]
+
+    v_far_p = [remote(slice_of(2, s), rq.at[0, s], yp) for s in (0, 1)]
+    v_far_m = [remote(slice_of(2, s + 2), rq.at[1, s], ym) for s in (0, 1)]
     g_p = remote(gbuf.at[:, 0], gbuf.at[:, 1], yp)
     g_m = remote(gbuf.at[:, 0], gbuf.at[:, 2], ym)
-    g_p.start()
-    g_m.start()
+    v_p = [remote(slice_of(1, s), rv.at[1, s, 0:24], yp) for s in range(4)]
+    v_m = [remote(slice_of(3, s), rv.at[2, s, 0:24], ym) for s in range(4)]
+    for one in (*v_far_p, *v_far_m, g_p, g_m, *v_p, *v_m):
+        one.start()
     g_in = remote(gx.at[:, 2 - core], gx.at[:, 3 * core], other)
     g_in.start()
     token_halo = [
@@ -223,39 +250,45 @@
     for copy, sent, _ in token_halo:
         pl.when(sent)(lambda copy=copy: copy.start())
 
-    loads[4].wait()
-    qf[...] = dot(vs[0:288, :], cols[...])
-
+    loads[5].wait()
     for copy, _, got in halo:
         pl.when(got)(lambda copy=copy: copy.wait_recv())
 
+    sub = lax.broadcasted_iota(jnp.int32, (16, 128), 0)
     lane = lax.broadcasted_iota(jnp.int32, (16, 128), 1)
-    for k, (a, b, d) in enumerate(((0, 2, 3), (1, 4, 5))):
-        hs[16 * k : 16 * k + 16, 0:256] = he[a, :, 0:256]
-        tile = jnp.where(
-            lane < 32, he[a, :, 256:384].astype(F32),
-            jnp.where(lane < 64, he[b, :, 256:384].astype(F32), he[d, :, 256:384].astype(F32)),
-        )
-        hs[16 * k : 16 * k + 16, 256:384] = tile.astype(BF16)
-    from_side = dot(hs[...], side[...], ((0,), (0,)))
-    qs[0:288, :] = (qf[...] + from_side[0:288]).astype(BF16)
-    qs[288:384, :] = (dot(hv[...], cols[...]) + from_side[288:384]).astype(BF16)
-    qw[...] = dot(rows[...], qs[...]).astype(BF16).reshape(12, 2, 16, 512)
-
-    for d, to in ((2, 2), (0, 1), (1, 3)):
-        for s in range(4):
-            at = chosen((y + to) % 4, [f[s] for f in FRAMES_OF])
-            sq[d, :, s] = qw[at]
-    q_far_p = remote(sq.at[2, :, 0:2], rq.at[0], yp)
-    q_far_m = remote(sq.at[2, :, 2:4], rq.at[1], ym)
-    q_p = remote(sq.at[0], qr.at[1], yp)
-    q_m = remote(sq.at[1], qr.at[2], ym)
-    for one in (q_far_p, q_far_m, q_p, q_m):
+    for n in range(3):
+        tile = slice(128 * n, 128 * n + 128)
+
+        def edge(beside_, above, below):
+            out = he[beside_, :, tile].astype(F32)
+            if n == 2:
+                out = jnp.where(
+                    lane < 32, out,
+                    jnp.where(lane < 64, he[above, :, tile].astype(F32), he[below, :, tile].astype(F32)),
+                )
+            return out
+
+        hs[:, tile] = jnp.where(sub < 2, edge(1, 4, 5), edge(0, 2, 3)).astype(BF16)
+    rim_rows = dot(rim_of[...], hv[...]).astype(BF16)
+    rim_cols = dot(hs[...], places[...]).astype(BF16)
+    for at in range(4):
+        ex[at, :, 0:384] = rim_rows[16 * at : 16 * at + 16]
+        ex[at, :, 384:512] = rim_cols[:, 128 * at : 128 * at + 128]
+    e_far = remote(ex.at[(y + 2) % 4], er.at[3], {"row": (r + 4) % 8})
+    e_p = remote(ex.at[(y + 1) % 4], er.at[1], yp)
+    e_m = remote(ex.at[(y + 3) % 4], er.at[2], ym)
+    for one in (e_far, e_p, e_m):
         one.start()
-    for s in range(4):
-        at = chosen(y, [f[s] for f in FRAMES_OF])
-        qr[0, :, s] = qw[at]
-
+    er[0] = ex[y]
+
+    for one in v_far_p:
+        one.wait_recv()
+    vf_p = remote(rq.at[0], rv.at[3, 0:2, 0:24], yp)
+    vf_p.start()
+    for one in v_far_m:
+        one.wait_recv()
+    vf_m = remote(rq.at[1], rv.at[3, 2:4, 0:24], ym)
+    vf_m.start()
     g_p.wait_recv()
     gf_p = remote(gbuf.at[0, 1], gbuf.at[0, 3], yp)
     gf_p.start()
@@ -271,7 +304,7 @@
     pl.when(g_got)(g_out.wait_recv)
     for copy, _, got in token_halo:
         pl.when(got)(lambda copy=copy: copy.wait_recv())
-    loads[5].wait()
+    loads[6].wait()
 
     ge[...] = dot(beside[...], hg[...].reshape(128, 512)).astype(BF16)
 
@@ -284,16 +317,7 @@
                 pg[2 * n, at, :] = block[:, 0:128]
                 pg[2 * n + 1, at, :] = block[:, 128:256]
 
-    token_grads(0, 6)
-
-    q_far_p.wait_recv()
-    qf_p = remote(rq.at[0], qr.at[3, :, 0:2], yp)
-    qf_p.start()
-    q_far_m.wait_recv()
-    qf_m = remote(rq.at[1], qr.at[3, :, 2:4], ym)
-    qf_m.start()
-
-    token_grads(6, 12)
+    token_grads(0, 12)
 
     def frames(e, first):
         early = pg[first, pl.ds(e, 192, stride=16), :].reshape(12, 16, 128)
@@ -342,12 +366,16 @@
     v_x = remote(ms, mr, partner)
     v_x.start()
 
-    for one in (q_p, q_m, qf_p, qf_m, gf_p, gf_m):
-        one.wait_recv()
+    def unfold(n):
+        at = dot(rv[n].reshape(128, 384), cols[...])
+        at = (at + dot(er[n, :, 384:512], side[...], ((0,), (0,)))).astype(BF16)
+        far = dot(er[n, :, 0:384], cols[...]).astype(BF16)
+        qr[n] = (dot(rows[...], at) + dot(rows_far[...], far)).astype(BF16).reshape(2, 4, 16, 512)
 
     block = lax.broadcasted_iota(jnp.int32, (64, 128), 1) // 32
-    for k in range(4):
-        for half in range(2):
+
+    def merge(half):
+        for k in range(4):
             parts = [
                 qr[2 * half + n // 2, n % 2, :, :, 128 * k : 128 * k + 128].astype(F32).reshape(64, 128)
                 for n in range(4)
@@ -359,6 +387,20 @@
                     part = pltpu.roll(parts[n], by, 1) if by else parts[n]
                     row = part if row is None else jnp.where(block == n, part, row)
                 lm[0:4, 4 * k + q, :, 128 * half : 128 * half + 128] = row.astype(BF16).reshape(4, 16, 128)
+
+    for k in range(7, 11):
+        loads[k].wait()
+    for one in (*v_p, *v_m, e_p, e_m):
+        one.wait_recv()
+    for n in range(3):
+        unfold(n)
+    merge(0)
+
+    for one in (vf_p, vf_m, e_far, gf_p, gf_m):
+        one.wait_recv()
+
+    unfold(3)
+    merge(1)
 
     give = []
     for p in range(PIECES):
@@ -432,7 +474,7 @@
 
     v_x.wait_recv()
     vg[m] = vg[m] + decoded(mr[16:160], mr[0:16].astype(F32)[0:1], (6, 24, 384))
-    v_out = pltpu.make_async_copy(vg.at[m], vout, load.at[6])
+    v_out = pltpu.make_async_copy(vg.at[m], vout, load.at[11])
     v_out.start()
 
     for p in range(PIECES):
@@ -446,7 +488,7 @@
         pl.when(sent)(lambda copy=copy: copy.wait_send())
     pl.when(g_sent)(g_out.wait_send)
     for one in (
-        g_p, g_m, g_in, gf_p, gf_m, q_far_p, q_far_m, q_p, q_m, qf_p, qf_m, v_x,
+        g_p, g_m, g_in, gf_p, gf_m, *v_far_p, *v_far_m, *v_p, *v_m, vf_p, vf_m, e_p, e_m, e_far, v_x,
         *give, *far, *near, *last, *sum(z_out, []),
     ):
         one.wait_send()
@@ -469,19 +511,20 @@
             jax.ShapeDtypeStruct((6, 24, 384), F32),
             jax.ShapeDtypeStruct((24, 512), F32),
         ),
-        in_specs=[anywhere] * 4,
+        in_specs=[anywhere] * 5,
         out_specs=(pl.BlockSpec(memory_space=pl.ANY), in_vmem),
         scratch_shapes=[
             b(SELECTION_ROWS, 512),
-            b(3072, 512), b(384, 384), b(96, 384), b(6, 16, 384), b(8, 16, 512), b(16, 384), b(16, 512), b(32, 384), v(288, 512),
-            b(2, 4, 32, 512), b(256, 512), b(2, 4, 2, 32, 512), b(384, 512), b(12, 2, 16, 512),
-            b(3, 2, 4, 16, 512), b(4, 2, 4, 16, 512), b(2, 2, 2, 16, 512), b(5, 16, 16, 256),
+            b(3072, 512), b(384, 384), b(12, 24, 384), b(4, 4, 32, 384), b(2, 2, 24, 384), b(64, 384),
+            b(6, 16, 384), b(8, 16, 512), b(16, 384), b(16, 512), b(16, 384), b(4, 16, 512), b(4, 16, 512),
+            b(2, 4, 32, 512), b(256, 512), b(2, 4, 2, 32, 512),
+            b(4, 2, 4, 16, 512), b(5, 16, 16, 256),
             v(4, 3072, 128), v(12, 12, 16, 128), b(768, 384), v(2, 6, 24, 384), b(160, 384), b(160, 384),
             v(4, 768, 128), v(4, 384, 128), v(4, 4, 4, 24, 128),
             *[b(2, PIECES, rows, 128) for rows in (CODED + 16, CODED + 16, CODED, CODED, CODED + 16, CODED + 16)],
             v(4, 4, 24, 128),
             v(3, 4, 24, 128),
-            pltpu.SemaphoreType.DMA((7,)),
+            pltpu.SemaphoreType.DMA((12,)),
             pltpu.SemaphoreType.DMA((N_SEMS,)),
             pltpu.SemaphoreType.DMA((N_SEMS,)),
         ],
@@ -489,7 +532,7 @@
             collective_id=0, has_side_effects=True, vmem_limit_bytes=VMEM_BYTES
         ),
         name="tubelet_backward",
-    )(video.reshape(288, 384), grad_tokens, weight, packed)
+    )(video.reshape(288, 384), video.reshape(12, 24, 384), grad_tokens, weight, packed)
     return video_grad.reshape(3, 2, 24, 384), weight_grad
 
 

time: 43.2 us -> 44.1 us (1.021)
  the two profiles are of different devices: /device:TPU:1 before, /device:TPU:2 now
where the time goes in v5:
time: 44.1 us; the launch traced here: 43.8 us
  Pallas kernels  40.9 us (93%)
  local copies, waits for them, and re-layouts  2.26 us (5%)
  between operations  0.64 us (1%)
    pallas_call x1, Pallas kernels, shards(): pl.pallas_call(kernel, out_shape=(jax.ShapeDtypeStruct((6, 24, 384), F32)...  40.9 us
    unnamed x2, local copies, waits for them, and re-layouts  2.26 us

profile of v5, /device:TPU:2, one launch (start us, length us, event | category | flops | bytes accessed | tf_op | source)
XLA Modules:
  0.0 43.8 jit_solution(12650532984283885701)
XLA Ops:
  0.6 40.9 %tubelet_backward.1 = (f32[6,24,384]{2,1,0:T(8,128)}, f32[24,512]{1,0:T(8,128)S(1)}) custom-call(bf16[288,384]{1,0:T(8,128)(2,1)} %bitcast.3, bf16[12,24,384]{2,1,0:T(8,128)(2,1)} %bitcast.4, bf16[2,2,32,512]{3,2,1,0:T(8,128)(2,1)} %tokens.1, bf16[3072,512]{1,0:T(8,128)(2,1)} %weight.1, bf16[1840,512]{1,0:T(8,128)(2,1)} %constant.2.clone.packed), custom_call_target="tpu_custom_call" | custom-call | tf_op jit(solution)/shard_map/tubelet_backward/pallas_call | solution.py:508
  41.5 1.6 %copy.8 = f32[3,2,24,384]{3,2,1,0:T(8,128)} copy(f32[3,2,24,384]{3,2,1,0:T(8,128)} %bitcast.5) | data formatting | bytes 442368
  43.2 0.6 %copy.9 = f32[24,512]{1,0:T(8,128)} copy(f32[24,512]{1,0:T(8,128)S(1)} %get-tuple-element.9) | data formatting | bytes 98304

commit v6 on v5

--- a/solution.py
+++ b/solution.py
@@ -15,8 +15,8 @@
 PIECES = 2
 WIDE = 4 // PIECES
 CODED = WIDE * 48
-SELECTION_AT = (0, 16, 80, 96, 480, 496, 880, 1008, 1136, 1200, 1456)
-SELECTION_ROWS = 1840
+SELECTION_AT = (0, 16, 80, 96, 480, 496, 880, 1008, 1136, 1200, 1328)
+SELECTION_ROWS = 1712
 
 
 def selections():
@@ -61,14 +61,14 @@
     for ti in range(4):
         ends[ti, ti * 32] = 1
         ends[4 + ti, ti * 32 + 31] = 1
-    beside = np.zeros((256, 128), np.float32)
+    beside = np.zeros((128, 128), np.float32)
     for t in range(2):
-        for i4 in range(4):
-            i = (1, 0, 1, 0)[i4]
-            left = (2, 0, 0, 3)[i4]
-            right = (4, 1, 1, 5)[i4]
-            beside[t * 128 + i4 * 32, left * 16 + 4 + t * 2 + i] = 1
-            beside[t * 128 + i4 * 32 + 31, right * 16 + t * 2 + i] = 1
+        for n in range(4):
+            i = (0, 1, 0, 1)[n]
+            left = (0, 0, 3, 2)[n]
+            right = (1, 1, 5, 4)[n]
+            beside[n * 32 + 16 * t, left * 16 + 4 + t * 2 + i] = 1
+            beside[n * 32 + 31 - 16 * t, right * 16 + t * 2 + i] = 1
     back = np.zeros((384, 384), np.float32)
     for e in range(12):
         for j in range(32):
@@ -132,7 +132,7 @@
     video, frames_h, tokens, weight, packed,
     vout, wout,
     sel,
-    wv, vs, v3, rv, rq, hv, he, hg, sb, sg, hs, ex, er, gx, ge, gbuf, qr, lm, pg, fs, ll, vg, ms, mr,
+    wv, vs, v3, rv, rq, hv, he, hg, sb, sg, hs, ex, er, gx, gh, gbuf, qr, lm, pg, fs, ll, vg, ms, mr,
     wg, cr, a1, fo, fi, no, ni, lo, li, a2, zr,
     load, send, recv,
 ):
@@ -143,7 +143,7 @@
     z, x = c // 4, c % 4
 
     pairs = [
-        (video, vs.at[0:288]), (packed.at[0:96], sel.at[0:96]), (tokens, gx.at[:, 1:3]),
+        (video, vs.at[0:288]), (packed.at[0:96], sel.at[0:96]), (tokens, gx.at[:, 0:2]),
         (tokens, gbuf.at[:, 0]), (frames_h, v3), (packed.at[96:SELECTION_ROWS], sel.at[96:SELECTION_ROWS]),
         (weight, wv),
     ]
@@ -156,14 +156,13 @@
     pick, rim, ends = sel.at[0:16, 0:384], sel.at[16:80, 0:288], sel.at[80:96, 0:128]
     cols, side, places = sel.at[96:480], sel.at[480:496], sel.at[496:880]
     rows, rows_far, rim_of = sel.at[880:1008, 0:128], sel.at[1008:1136, 0:16], sel.at[1136:1200, 0:64]
-    beside, back = sel.at[1200:1456, 0:128], sel.at[1456:1840, 0:384]
+    beside, back = sel.at[1200:1328, 0:128], sel.at[1328:1712, 0:384]
 
     hv[...] = jnp.zeros_like(hv)
     he[...] = jnp.zeros_like(he)
     hg[...] = jnp.zeros_like(hg)
     vs[288:384, :] = jnp.zeros((96, 384), BF16)
-    for i4 in (0, 3):
-        gx[:, i4] = jnp.zeros((2, 32, 512), BF16)
+    gx[:, 2:4] = jnp.zeros((2, 2, 32, 512), BF16)
     rv[:, :, 24:32] = jnp.zeros((4, 4, 8, 384), BF16)
     lm[4] = jnp.zeros((16, 16, 256), BF16)
 
@@ -206,7 +205,7 @@
         loads[k].wait()
     vs[288:352, :] = dot(rim[...], vs[0:288, :]).astype(BF16)
     sb[...] = dot(pick[...], vs[...], ((1,), (1,))).astype(BF16)
-    sg[...] = dot(ends[...], gx[:, 1:3].reshape(128, 512)).astype(BF16)
+    sg[...] = dot(ends[...], gx[:, 0:2].reshape(128, 512)).astype(BF16)
     loads[3].wait()
     loads[4].wait()
 
@@ -235,9 +234,9 @@
     g_m = remote(gbuf.at[:, 0], gbuf.at[:, 2], ym)
     v_p = [remote(slice_of(1, s), rv.at[1, s, 0:24], yp) for s in range(4)]
     v_m = [remote(slice_of(3, s), rv.at[2, s, 0:24], ym) for s in range(4)]
-    for one in (*v_far_p, *v_far_m, g_p, g_m, *v_p, *v_m):
+    for one in (g_p, g_m, *v_far_p, *v_far_m, *v_p, *v_m):
         one.start()
-    g_in = remote(gx.at[:, 2 - core], gx.at[:, 3 * core], other)
+    g_in = remote(gx.at[:, 1 - core], gx.at[:, 3 - core], other)
     g_in.start()
     token_halo = [
         (remote(sg, hg.at[0], {"col": c + 1}), rig, lef),
@@ -249,6 +248,13 @@
     ]
     for copy, sent, _ in token_halo:
         pl.when(sent)(lambda copy=copy: copy.start())
+
+    loads[6].wait()
+
+    @pl.loop(0, 12)
+    def _(k):
+        at = pl.ds(pl.multiple_of(k * 256, 256), 256)
+        pg[0, at, :] = dot(wv[at, :], gx[:, 0:2].reshape(128, 512), ((1,), (1,)))
 
     loads[5].wait()
     for copy, _, got in halo:
@@ -280,91 +286,6 @@
     for one in (e_far, e_p, e_m):
         one.start()
     er[0] = ex[y]
-
-    for one in v_far_p:
-        one.wait_recv()
-    vf_p = remote(rq.at[0], rv.at[3, 0:2, 0:24], yp)
-    vf_p.start()
-    for one in v_far_m:
-        one.wait_recv()
-    vf_m = remote(rq.at[1], rv.at[3, 2:4, 0:24], ym)
-    vf_m.start()
-    g_p.wait_recv()
-    gf_p = remote(gbuf.at[0, 1], gbuf.at[0, 3], yp)
-    gf_p.start()
-    g_m.wait_recv()
-    gf_m = remote(gbuf.at[1, 2], gbuf.at[1, 3], ym)
-    gf_m.start()
-    g_out = remote(gbuf.at[:, 2 - core, core], gx.at[:, 3 - 3 * core], other)
-    g_sent = ((core == 0) & (y < 3)) | ((core == 1) & (y > 0))
-    g_got = ((core == 0) & (y > 0)) | ((core == 1) & (y < 3))
-    pl.when(g_sent)(g_out.start)
-
-    g_in.wait_recv()
-    pl.when(g_got)(g_out.wait_recv)
-    for copy, _, got in token_halo:
-        pl.when(got)(lambda copy=copy: copy.wait_recv())
-    loads[6].wait()
-
-    ge[...] = dot(beside[...], hg[...].reshape(128, 512)).astype(BF16)
-
-    def token_grads(first, last):
-        @pl.loop(first, last)
-        def _(k):
-            at = pl.ds(pl.multiple_of(k * 256, 256), 256)
-            for n, right in enumerate((gx[...].reshape(256, 512), ge[...])):
-                block = dot(wv[at, :], right, ((1,), (1,)))
-                pg[2 * n, at, :] = block[:, 0:128]
-                pg[2 * n + 1, at, :] = block[:, 128:256]
-
-    token_grads(0, 12)
-
-    def frames(e, first):
-        early = pg[first, pl.ds(e, 192, stride=16), :].reshape(12, 16, 128)
-        late = pg[first + 1, pl.ds(e, 192, stride=16), :].reshape(12, 16, 128)
-        out = []
-        for ch in range(0, 12, 4):
-            out += [
-                early[ch + 1], early[ch + 2] + late[ch], early[ch + 3] + late[ch + 1], late[ch + 2],
-            ]
-        return jnp.stack(out)
-
-    j = lax.broadcasted_iota(jnp.int32, (12, 16, 128), 2) % 32
-    sub = lax.broadcasted_iota(jnp.int32, (12, 8, 128), 1)
-    wrap = {0: (14, 0, 1), 1: (15, 0, 1), 10: (0, 31, 127), 11: (1, 31, 127)}
-    for e in range(12):
-        cell = frames(e + 2, 0)
-        if e in wrap:
-            far, at, by = wrap[e]
-            cell = cell + jnp.where(j == at, frames(far, 2), pltpu.roll(frames(far, 0), by, 2))
-        low, high = cell[:, 0:8], cell[:, 8:16]
-        to_low = pltpu.roll(pltpu.roll(high, 32, 2), 4, 1)
-        to_high = pltpu.roll(pltpu.roll(low, 96, 2), 4, 1)
-        fs[e, :, 0:8] = low + jnp.where((sub == 2) | (sub == 3), to_low, 0.0)
-        fs[e, :, 8:16] = high + jnp.where((sub == 4) | (sub == 5), to_high, 0.0)
-    block = lax.broadcasted_iota(jnp.int32, (192, 128), 1) // 32
-    for i in range(2):
-        for k in range(3):
-            row = None
-            for q in range(4):
-                part = fs[4 * k + q].reshape(192, 128)
-                by = ((q - i - 1) * 32) % 128
-                if by:
-                    part = pltpu.roll(part, by, 1)
-                row = part if row is None else jnp.where(block == q, part, row)
-            upper = row.astype(BF16)
-            ll[192 * i : 192 * i + 192, 128 * k : 128 * k + 128] = upper
-            ll[384 + 192 * i : 576 + 192 * i, 128 * k : 128 * k + 128] = (row - upper.astype(F32)).astype(BF16)
-    pixels = (dot(ll[0:384, :], back[...]) + dot(ll[384:768, :], back[...])).reshape(2, 12, 16, 384)
-    for i in range(2):
-        for cf in range(12):
-            ch, f = cf // 4, cf % 4
-            vg[f // 2, ch * 2 + f % 2, 12 * i : 12 * i + 12, :] = pixels[i, cf, 2:14, :]
-    top = largest(vg[1 - m])
-    ms[0:16] = spread(top, 384)
-    ms[16:160] = coded(vg[1 - m], top)
-    v_x = remote(ms, mr, partner)
-    v_x.start()
 
     def unfold(n):
         at = dot(rv[n].reshape(128, 384), cols[...])
@@ -390,12 +311,85 @@
 
     for k in range(7, 11):
         loads[k].wait()
+    unfold(0)
+
+    g_p.wait_recv()
+    gf_p = remote(gbuf.at[0, 1], gbuf.at[0, 3], yp)
+    gf_p.start()
+    g_m.wait_recv()
+    gf_m = remote(gbuf.at[1, 2], gbuf.at[1, 3], ym)
+    gf_m.start()
+    g_out = remote(gbuf.at[:, 2 - core, core], gx.at[:, 2 + core], other)
+    g_sent = ((core == 0) & (y < 3)) | ((core == 1) & (y > 0))
+    g_got = ((core == 0) & (y > 0)) | ((core == 1) & (y < 3))
+    pl.when(g_sent)(g_out.start)
+
+    for one in v_far_p:
+        one.wait_recv()
+    vf_p = remote(rq.at[0], rv.at[3, 0:2, 0:24], yp)
+    vf_p.start()
+    for one in v_far_m:
+        one.wait_recv()
+    vf_m = remote(rq.at[1], rv.at[3, 2:4, 0:24], ym)
+    vf_m.start()
+
+    g_in.wait_recv()
+    pl.when(g_got)(g_out.wait_recv)
+    for copy, _, got in token_halo:
+        pl.when(got)(lambda copy=copy: copy.wait_recv())
+
+    gh[0:128] = gx[:, 2:4].reshape(128, 512)
+    gh[128:256] = dot(beside[...], hg[...].reshape(128, 512)).astype(BF16)
+
+    @pl.loop(0, 12)
+    def _(k):
+        at = pl.ds(pl.multiple_of(k * 256, 256), 256)
+        out = dot(wv[at, :], gh[...], ((1,), (1,)))
+        pg[1, at, :] = out[:, 0:128]
+        pg[2, at, :] = out[:, 128:256]
+
     for one in (*v_p, *v_m, e_p, e_m):
         one.wait_recv()
-    for n in range(3):
-        unfold(n)
+    unfold(1)
+    unfold(2)
     merge(0)
 
+    first = lax.broadcasted_iota(jnp.int32, (12, 16, 128), 2) < 64
+
+    def summed(early, late):
+        out = []
+        for ch in range(0, 12, 4):
+            out += [
+                early[ch + 1], early[ch + 2] + late[ch], early[ch + 3] + late[ch + 1], late[ch + 2],
+            ]
+        return jnp.stack(out)
+
+    def rows_of(n, e):
+        return pg[n, pl.ds(e, 192, stride=16), :].reshape(12, 16, 128)
+
+    def frames(e):
+        own, around = rows_of(0, e), rows_of(1, e)
+        return summed(
+            jnp.where(first, own, pltpu.roll(around, 64, 2)), jnp.where(first, pltpu.roll(own, 64, 2), around)
+        )
+
+    def frames_beside(e):
+        both = rows_of(2, e)
+        return summed(both, pltpu.roll(both, 16 if e < 8 else 112, 2))
+
+    j = lax.broadcasted_iota(jnp.int32, (12, 16, 128), 2) % 32
+    sub = lax.broadcasted_iota(jnp.int32, (12, 8, 128), 1)
+    wrap = {0: (14, 0, 1), 1: (15, 0, 1), 10: (0, 31, 127), 11: (1, 31, 127)}
+    for e in range(12):
+        cell = frames(e + 2)
+        if e in wrap:
+            far, at, by = wrap[e]
+            cell = cell + jnp.where(j == at, frames_beside(far), pltpu.roll(frames(far), by, 2))
+        low, high = cell[:, 0:8], cell[:, 8:16]
+        to_low = pltpu.roll(pltpu.roll(high, 32, 2), 4, 1)
+        to_high = pltpu.roll(pltpu.roll(low, 96, 2), 4, 1)
+        fs[e, :, 0:8] = low + jnp.where((sub == 2) | (sub == 3), to_low, 0.0)
+        fs[e, :, 8:16] = high + jnp.where((sub == 4) | (sub == 5), to_high, 0.0)
     for one in (vf_p, vf_m, e_far, gf_p, gf_m):
         one.wait_recv()
 
@@ -419,6 +413,30 @@
         tiles = slice(WIDE * p, WIDE * p + WIDE)
         give.append(remote(wg.at[tiles, pl.ds((1 - core) * 384, 384)], cr.at[tiles], other))
         give[p].start()
+
+    block = lax.broadcasted_iota(jnp.int32, (192, 128), 1) // 32
+    for i in range(2):
+        for k in range(3):
+            row = None
+            for q in range(4):
+                part = fs[4 * k + q].reshape(192, 128)
+                by = ((q - i) * 32) % 128
+                if by:
+                    part = pltpu.roll(part, by, 1)
+                row = part if row is None else jnp.where(block == q, part, row)
+            upper = row.astype(BF16)
+            ll[192 * i : 192 * i + 192, 128 * k : 128 * k + 128] = upper
+            ll[384 + 192 * i : 576 + 192 * i, 128 * k : 128 * k + 128] = (row - upper.astype(F32)).astype(BF16)
+    pixels = (dot(ll[0:384, :], back[...]) + dot(ll[384:768, :], back[...])).reshape(2, 12, 16, 384)
+    for i in range(2):
+        for cf in range(12):
+            ch, f = cf // 4, cf % 4
+            vg[f // 2, ch * 2 + f % 2, 12 * i : 12 * i + 12, :] = pixels[i, cf, 2:14, :]
+    top = largest(vg[1 - m])
+    ms[0:16] = spread(top, 384)
+    ms[16:160] = coded(vg[1 - m], top)
+    v_x = remote(ms, mr, partner)
+    v_x.start()
 
     x1, x2, x3 = (x + 1) % 4, (x + 2) % 4, (x + 3) % 4
     far, near, last, tops = [], [], [], []
@@ -519,7 +537,7 @@
             b(6, 16, 384), b(8, 16, 512), b(16, 384), b(16, 512), b(16, 384), b(4, 16, 512), b(4, 16, 512),
             b(2, 4, 32, 512), b(256, 512), b(2, 4, 2, 32, 512),
             b(4, 2, 4, 16, 512), b(5, 16, 16, 256),
-            v(4, 3072, 128), v(12, 12, 16, 128), b(768, 384), v(2, 6, 24, 384), b(160, 384), b(160, 384),
+            v(3, 3072, 128), v(12, 12, 16, 128), b(768, 384), v(2, 6, 24, 384), b(160, 384), b(160, 384),
             v(4, 768, 128), v(4, 384, 128), v(4, 4, 4, 24, 128),
             *[b(2, PIECES, rows, 128) for rows in (CODED + 16, CODED + 16, CODED, CODED, CODED + 16, CODED + 16)],
             v(4, 4, 24, 128),

time: 44.1 us -> 43.8 us (level)
  the two profiles are of different devices: /device:TPU:2 before, /device:TPU:1 now
where the time goes in v6:
time: 43.8 us; the launch traced here: 43.7 us
  Pallas kernels  40.8 us (93%)
  local copies, waits for them, and re-layouts  2.26 us (5%)
  between operations  0.64 us (1%)
    pallas_call x1, Pallas kernels, shards(): pl.pallas_call(kernel, out_shape=(jax.ShapeDtypeStruct((6, 24, 384), F32)...  40.8 us
    unnamed x2, local copies, waits for them, and re-layouts  2.26 us

profile of v6, /device:TPU:1, one launch (start us, length us, event | category | flops | bytes accessed | tf_op | source)
XLA Modules:
  0.0 43.7 jit_solution(16251626018294449806)
XLA Ops:
  0.6 40.8 %tubelet_backward.1 = (f32[6,24,384]{2,1,0:T(8,128)}, f32[24,512]{1,0:T(8,128)S(1)}) custom-call(bf16[288,384]{1,0:T(8,128)(2,1)} %bitcast.3, bf16[12,24,384]{2,1,0:T(8,128)(2,1)} %bitcast.4, bf16[2,2,32,512]{3,2,1,0:T(8,128)(2,1)} %tokens.1, bf16[3072,512]{1,0:T(8,128)(2,1)} %weight.1, bf16[1712,512]{1,0:T(8,128)(2,1)} %constant.2.clone.packed), custom_call_target="tpu_custom_call" | custom-call | tf_op jit(solution)/shard_map/tubelet_backward/pallas_call | solution.py:526
  41.5 1.6 %copy.8 = f32[3,2,24,384]{3,2,1,0:T(8,128)} copy(f32[3,2,24,384]{3,2,1,0:T(8,128)} %bitcast.5) | data formatting | bytes 442368
  43.1 0.6 %copy.9 = f32[24,512]{1,0:T(8,128)} copy(f32[24,512]{1,0:T(8,128)S(1)} %get-tuple-element.9) | data formatting | bytes 98304

commit v7 on v6

--- a/solution.py
+++ b/solution.py
@@ -10,13 +10,14 @@
 F32 = jnp.float32
 BF16 = jnp.bfloat16
 N_SEMS = 80
+TALL = 1536
 FRAMES_OF = ((0, 1, 2, 3), (2, 4, 5, 6), (5, 6, 7, 9), (8, 9, 10, 11))
 VMEM_BYTES = 56500000
 PIECES = 2
 WIDE = 4 // PIECES
 CODED = WIDE * 48
-SELECTION_AT = (0, 16, 80, 96, 480, 496, 880, 1008, 1136, 1200, 1328)
-SELECTION_ROWS = 1712
+SELECTION_AT = (0, 16, 80, 96, 480, 496, 880, 1008, 1072, 1200)
+SELECTION_ROWS = 1584
 
 
 def selections():
@@ -39,8 +40,7 @@
                 far = (k // 2) * 32 + cf * 2 + k % 2
                 rim_of[at * 16 + s * 4 + k, far] = 1
                 places[288 + far, at * 128 + s * 32 + 24 + k] = 1
-    rows = np.zeros((128, 128), np.float32)
-    rows_far = np.zeros((128, 16), np.float32)
+    rows = np.zeros((128, 144), np.float32)
     for i in range(2):
         for s in range(4):
             for b in range(16):
@@ -48,7 +48,7 @@
                 k = y + 2 if y < 0 else y - 22
                 rows[i * 64 + s * 16 + b, s * 32 + (y if 0 <= y < 24 else 24 + k)] = 1
                 if not 0 <= y < 24:
-                    rows_far[i * 64 + s * 16 + b, s * 4 + k] = 1
+                    rows[i * 64 + s * 16 + b, 128 + s * 4 + k] = 1
     pick = np.zeros((16, 384), np.float32)
     for k, x in enumerate((0, 1, 382, 383)):
         pick[k, x] = 1
@@ -74,7 +74,7 @@
         for j in range(32):
             back[e * 32 + j, 12 * j + e] = 1
     packed = np.zeros((SELECTION_ROWS, 512), np.float32)
-    for at, one in zip(SELECTION_AT, (pick, rim, ends, cols, side, places, rows, rows_far, rim_of, beside, back)):
+    for at, one in zip(SELECTION_AT, (pick, rim, ends, cols, side, places, rows, rim_of, beside, back)):
         packed[at : at + one.shape[0], : one.shape[1]] = one
     return packed
 
@@ -132,7 +132,7 @@
     video, frames_h, tokens, weight, packed,
     vout, wout,
     sel,
-    wv, vs, v3, rv, rq, hv, he, hg, sb, sg, hs, ex, er, gx, gh, gbuf, qr, lm, pg, fs, ll, vg, ms, mr,
+    wv, vs, v3, rv, rq, hv, he, hg, sb, sg, hs, ex, er, gx, gh, gbuf, qs, qr, lm, pg, fs, ll, vg, ms, mr,
     wg, cr, a1, fo, fi, no, ni, lo, li, a2, zr,
     load, send, recv,
 ):
@@ -155,8 +155,8 @@
 
     pick, rim, ends = sel.at[0:16, 0:384], sel.at[16:80, 0:288], sel.at[80:96, 0:128]
     cols, side, places = sel.at[96:480], sel.at[480:496], sel.at[496:880]
-    rows, rows_far, rim_of = sel.at[880:1008, 0:128], sel.at[1008:1136, 0:16], sel.at[1136:1200, 0:64]
-    beside, back = sel.at[1200:1328, 0:128], sel.at[1328:1712, 0:384]
+    rows, rim_of = sel.at[880:1008, 0:144], sel.at[1008:1072, 0:64]
+    beside, back = sel.at[1072:1200, 0:128], sel.at[1200:1584, 0:384]
 
     hv[...] = jnp.zeros_like(hv)
     he[...] = jnp.zeros_like(he)
@@ -251,10 +251,12 @@
 
     loads[6].wait()
 
-    @pl.loop(0, 12)
+    @pl.loop(0, 3072 // TALL)
     def _(k):
-        at = pl.ds(pl.multiple_of(k * 256, 256), 256)
-        pg[0, at, :] = dot(wv[at, :], gx[:, 0:2].reshape(128, 512), ((1,), (1,)))
+        at = pl.ds(pl.multiple_of(k * TALL, TALL), TALL)
+        out = dot(wv[at, :], gx[:, 0:2].reshape(128, 512), ((1,), (1,)))
+        pg[0, at, 0:64] = out[:, 0:64]
+        pg[1, at, 0:64] = pltpu.roll(out, 64, 1)[:, 0:64]
 
     loads[5].wait()
     for copy, _, got in halo:
@@ -287,11 +289,16 @@
         one.start()
     er[0] = ex[y]
 
-    def unfold(n):
-        at = dot(rv[n].reshape(128, 384), cols[...])
-        at = (at + dot(er[n, :, 384:512], side[...], ((0,), (0,)))).astype(BF16)
-        far = dot(er[n, :, 0:384], cols[...]).astype(BF16)
-        qr[n] = (dot(rows[...], at) + dot(rows_far[...], far)).astype(BF16).reshape(2, 4, 16, 512)
+    def unfold(*sources):
+        pixels = []
+        for n in sources:
+            pixels += [rv[n].reshape(128, 384), er[n, :, 0:384]]
+        at = dot(jnp.concatenate(pixels, axis=0), cols[...])
+        for k, n in enumerate(sources):
+            from_side = dot(er[n, :, 384:512], side[...], ((0,), (0,)))
+            qs[0:128] = (at[144 * k : 144 * k + 128] + from_side).astype(BF16)
+            qs[128:144] = at[144 * k + 128 : 144 * k + 144].astype(BF16)
+            qr[n] = dot(rows[...], qs[...]).astype(BF16).reshape(2, 4, 16, 512)
 
     block = lax.broadcasted_iota(jnp.int32, (64, 128), 1) // 32
 
@@ -341,20 +348,18 @@
     gh[0:128] = gx[:, 2:4].reshape(128, 512)
     gh[128:256] = dot(beside[...], hg[...].reshape(128, 512)).astype(BF16)
 
-    @pl.loop(0, 12)
+    @pl.loop(0, 3072 // TALL)
     def _(k):
-        at = pl.ds(pl.multiple_of(k * 256, 256), 256)
+        at = pl.ds(pl.multiple_of(k * TALL, TALL), TALL)
         out = dot(wv[at, :], gh[...], ((1,), (1,)))
-        pg[1, at, :] = out[:, 0:128]
+        pg[0, at, 64:128] = pltpu.roll(out[:, 0:128], 64, 1)[:, 64:128]
+        pg[1, at, 64:128] = out[:, 64:128]
         pg[2, at, :] = out[:, 128:256]
 
     for one in (*v_p, *v_m, e_p, e_m):
         one.wait_recv()
-    unfold(1)
-    unfold(2)
+    unfold(1, 2)
     merge(0)
-
-    first = lax.broadcasted_iota(jnp.int32, (12, 16, 128), 2) < 64
 
     def summed(early, late):
         out = []
@@ -368,10 +373,7 @@
         return pg[n, pl.ds(e, 192, stride=16), :].reshape(12, 16, 128)
 
     def frames(e):
-        own, around = rows_of(0, e), rows_of(1, e)
-        return summed(
-            jnp.where(first, own, pltpu.roll(around, 64, 2)), jnp.where(first, pltpu.roll(own, 64, 2), around)
-        )
+        return summed(rows_of(0, e), rows_of(1, e))
 
     def frames_beside(e):
         both = rows_of(2, e)
@@ -427,7 +429,8 @@
             upper = row.astype(BF16)
             ll[192 * i : 192 * i + 192, 128 * k : 128 * k + 128] = upper
             ll[384 + 192 * i : 576 + 192 * i, 128 * k : 128 * k + 128] = (row - upper.astype(F32)).astype(BF16)
-    pixels = (dot(ll[0:384, :], back[...]) + dot(ll[384:768, :], back[...])).reshape(2, 12, 16, 384)
+    pixels = dot(ll[...], back[...])
+    pixels = (pixels[0:384] + pixels[384:768]).reshape(2, 12, 16, 384)
     for i in range(2):
         for cf in range(12):
             ch, f = cf // 4, cf % 4
@@ -535,7 +538,7 @@
             b(SELECTION_ROWS, 512),
             b(3072, 512), b(384, 384), b(12, 24, 384), b(4, 4, 32, 384), b(2, 2, 24, 384), b(64, 384),
             b(6, 16, 384), b(8, 16, 512), b(16, 384), b(16, 512), b(16, 384), b(4, 16, 512), b(4, 16, 512),
-            b(2, 4, 32, 512), b(256, 512), b(2, 4, 2, 32, 512),
+            b(2, 4, 32, 512), b(256, 512), b(2, 4, 2, 32, 512), b(144, 512),
             b(4, 2, 4, 16, 512), b(5, 16, 16, 256),
             v(3, 3072, 128), v(12, 12, 16, 128), b(768, 384), v(2, 6, 24, 384), b(160, 384), b(160, 384),
             v(4, 768, 128), v(4, 384, 128), v(4, 4, 4, 24, 128),

time: 43.8 us -> 40.1 us (0.916)
  the two profiles are of different devices: /device:TPU:1 before, /device:TPU:2 now
where the time goes in v7:
time: 40.1 us; the launch traced here: 39.4 us
  Pallas kernels  36.5 us (91%)
  local copies, waits for them, and re-layouts  2.26 us (6%)
  between operations  0.64 us (2%)
    pallas_call x1, Pallas kernels, shards(): pl.pallas_call(kernel, out_shape=(jax.ShapeDtypeStruct((6, 24, 384), F32)...  36.5 us
    unnamed x2, local copies, waits for them, and re-layouts  2.26 us

profile of v7, /device:TPU:2, one launch (start us, length us, event | category | flops | bytes accessed | tf_op | source)
XLA Modules:
  0.0 39.4 jit_solution(16124714919873994497)
XLA Ops:
  0.6 36.5 %tubelet_backward.1 = (f32[6,24,384]{2,1,0:T(8,128)}, f32[24,512]{1,0:T(8,128)S(1)}) custom-call(bf16[288,384]{1,0:T(8,128)(2,1)} %bitcast.3, bf16[12,24,384]{2,1,0:T(8,128)(2,1)} %bitcast.4, bf16[2,2,32,512]{3,2,1,0:T(8,128)(2,1)} %tokens.1, bf16[3072,512]{1,0:T(8,128)(2,1)} %weight.1, bf16[1584,512]{1,0:T(8,128)(2,1)} %constant.2.clone.packed), custom_call_target="tpu_custom_call" | custom-call | tf_op jit(solution)/shard_map/tubelet_backward/pallas_call | solution.py:529
  37.1 1.6 %copy.8 = f32[3,2,24,384]{3,2,1,0:T(8,128)} copy(f32[3,2,24,384]{3,2,1,0:T(8,128)} %bitcast.5) | data formatting | bytes 442368
  38.8 0.6 %copy.9 = f32[24,512]{1,0:T(8,128)} copy(f32[24,512]{1,0:T(8,128)S(1)} %get-tuple-element.9) | data formatting | bytes 98304

commit v8 on v7

--- a/solution.py
+++ b/solution.py
@@ -225,16 +225,23 @@
     for copy, sent, _ in halo:
         pl.when(sent)(lambda copy=copy: copy.start())
 
+    g_sent = ((core == 1) & down) | ((core == 0) & up)
+    g_got = ((core == 0) & up) | ((core == 1) & down)
+    g_out = remote(gx.at[:, core], gx.at[:, 2 + core], {"row": r + 2 * core - 1})
+
     def slice_of(to, s):
         return v3.at[chosen((y + to) % 4, [f[s] for f in FRAMES_OF])]
 
     v_far_p = [remote(slice_of(2, s), rq.at[0, s], yp) for s in (0, 1)]
     v_far_m = [remote(slice_of(2, s + 2), rq.at[1, s], ym) for s in (0, 1)]
-    g_p = remote(gbuf.at[:, 0], gbuf.at[:, 1], yp)
-    g_m = remote(gbuf.at[:, 0], gbuf.at[:, 2], ym)
+    g_p = [remote(gbuf.at[t, 0], gbuf.at[t, 1], yp) for t in (0, 1)]
+    g_m = [remote(gbuf.at[t, 0], gbuf.at[t, 2], ym) for t in (1, 0)]
     v_p = [remote(slice_of(1, s), rv.at[1, s, 0:24], yp) for s in range(4)]
     v_m = [remote(slice_of(3, s), rv.at[2, s, 0:24], ym) for s in range(4)]
-    for one in (g_p, g_m, *v_far_p, *v_far_m, *v_p, *v_m):
+    for one in (g_p[0], g_m[0]):
+        one.start()
+    pl.when(g_sent)(g_out.start)
+    for one in (*v_far_p, *v_far_m, g_p[1], g_m[1], *v_p, *v_m):
         one.start()
     g_in = remote(gx.at[:, 1 - core], gx.at[:, 3 - core], other)
     g_in.start()
@@ -320,16 +327,28 @@
         loads[k].wait()
     unfold(0)
 
-    g_p.wait_recv()
+    g_in.wait_recv()
+    pl.when(g_got)(g_out.wait_recv)
+    for copy, _, got in token_halo:
+        pl.when(got)(lambda copy=copy: copy.wait_recv())
+
+    gh[0:128] = gx[:, 2:4].reshape(128, 512)
+    gh[128:256] = dot(beside[...], hg[...].reshape(128, 512)).astype(BF16)
+
+    @pl.loop(0, 3072 // TALL)
+    def _(k):
+        at = pl.ds(pl.multiple_of(k * TALL, TALL), TALL)
+        out = dot(wv[at, :], gh[...], ((1,), (1,)))
+        pg[0, at, 64:128] = pltpu.roll(out[:, 0:128], 64, 1)[:, 64:128]
+        pg[1, at, 64:128] = out[:, 64:128]
+        pg[2, at, :] = out[:, 128:256]
+
+    g_p[0].wait_recv()
     gf_p = remote(gbuf.at[0, 1], gbuf.at[0, 3], yp)
     gf_p.start()
-    g_m.wait_recv()
+    g_m[0].wait_recv()
     gf_m = remote(gbuf.at[1, 2], gbuf.at[1, 3], ym)
     gf_m.start()
-    g_out = remote(gbuf.at[:, 2 - core, core], gx.at[:, 2 + core], other)
-    g_sent = ((core == 0) & (y < 3)) | ((core == 1) & (y > 0))
-    g_got = ((core == 0) & (y > 0)) | ((core == 1) & (y < 3))
-    pl.when(g_sent)(g_out.start)
 
     for one in v_far_p:
         one.wait_recv()
@@ -339,27 +358,6 @@
         one.wait_recv()
     vf_m = remote(rq.at[1], rv.at[3, 2:4, 0:24], ym)
     vf_m.start()
-
-    g_in.wait_recv()
-    pl.when(g_got)(g_out.wait_recv)
-    for copy, _, got in token_halo:
-        pl.when(got)(lambda copy=copy: copy.wait_recv())
-
-    gh[0:128] = gx[:, 2:4].reshape(128, 512)
-    gh[128:256] = dot(beside[...], hg[...].reshape(128, 512)).astype(BF16)
-
-    @pl.loop(0, 3072 // TALL)
-    def _(k):
-        at = pl.ds(pl.multiple_of(k * TALL, TALL), TALL)
-        out = dot(wv[at, :], gh[...], ((1,), (1,)))
-        pg[0, at, 64:128] = pltpu.roll(out[:, 0:128], 64, 1)[:, 64:128]
-        pg[1, at, 64:128] = out[:, 64:128]
-        pg[2, at, :] = out[:, 128:256]
-
-    for one in (*v_p, *v_m, e_p, e_m):
-        one.wait_recv()
-    unfold(1, 2)
-    merge(0)
 
     def summed(early, late):
         out = []
@@ -392,7 +390,37 @@
         to_high = pltpu.roll(pltpu.roll(low, 96, 2), 4, 1)
         fs[e, :, 0:8] = low + jnp.where((sub == 2) | (sub == 3), to_low, 0.0)
         fs[e, :, 8:16] = high + jnp.where((sub == 4) | (sub == 5), to_high, 0.0)
-    for one in (vf_p, vf_m, e_far, gf_p, gf_m):
+    quarter = lax.broadcasted_iota(jnp.int32, (192, 128), 1) // 32
+    for i in range(2):
+        for k in range(3):
+            row = None
+            for q in range(4):
+                part = fs[4 * k + q].reshape(192, 128)
+                by = ((q - i) * 32) % 128
+                if by:
+                    part = pltpu.roll(part, by, 1)
+                row = part if row is None else jnp.where(quarter == q, part, row)
+            upper = row.astype(BF16)
+            ll[192 * i : 192 * i + 192, 128 * k : 128 * k + 128] = upper
+            ll[384 + 192 * i : 576 + 192 * i, 128 * k : 128 * k + 128] = (row - upper.astype(F32)).astype(BF16)
+    pixels = dot(ll[...], back[...])
+    pixels = (pixels[0:384] + pixels[384:768]).reshape(2, 12, 16, 384)
+    for i in range(2):
+        for cf in range(12):
+            ch, f = cf // 4, cf % 4
+            vg[f // 2, ch * 2 + f % 2, 12 * i : 12 * i + 12, :] = pixels[i, cf, 2:14, :]
+    top = largest(vg[1 - m])
+    ms[0:16] = spread(top, 384)
+    ms[16:160] = coded(vg[1 - m], top)
+    v_x = remote(ms, mr, partner)
+    v_x.start()
+
+    for one in (*v_p, *v_m, e_p, e_m):
+        one.wait_recv()
+    unfold(1, 2)
+    merge(0)
+
+    for one in (vf_p, vf_m, e_far, g_p[1], g_m[1], gf_p, gf_m):
         one.wait_recv()
 
     unfold(3)
@@ -415,31 +443,6 @@
         tiles = slice(WIDE * p, WIDE * p + WIDE)
         give.append(remote(wg.at[tiles, pl.ds((1 - core) * 384, 384)], cr.at[tiles], other))
         give[p].start()
-
-    block = lax.broadcasted_iota(jnp.int32, (192, 128), 1) // 32
-    for i in range(2):
-        for k in range(3):
-            row = None
-            for q in range(4):
-                part = fs[4 * k + q].reshape(192, 128)
-                by = ((q - i) * 32) % 128
-                if by:
-                    part = pltpu.roll(part, by, 1)
-                row = part if row is None else jnp.where(block == q, part, row)
-            upper = row.astype(BF16)
-            ll[192 * i : 192 * i + 192, 128 * k : 128 * k + 128] = upper
-            ll[384 + 192 * i : 576 + 192 * i, 128 * k : 128 * k + 128] = (row - upper.astype(F32)).astype(BF16)
-    pixels = dot(ll[...], back[...])
-    pixels = (pixels[0:384] + pixels[384:768]).reshape(2, 12, 16, 384)
-    for i in range(2):
-        for cf in range(12):
-            ch, f = cf // 4, cf % 4
-            vg[f // 2, ch * 2 + f % 2, 12 * i : 12 * i + 12, :] = pixels[i, cf, 2:14, :]
-    top = largest(vg[1 - m])
-    ms[0:16] = spread(top, 384)
-    ms[16:160] = coded(vg[1 - m], top)
-    v_x = remote(ms, mr, partner)
-    v_x.start()
 
     x1, x2, x3 = (x + 1) % 4, (x + 2) % 4, (x + 3) % 4
     far, near, last, tops = [], [], [], []
@@ -509,7 +512,7 @@
         pl.when(sent)(lambda copy=copy: copy.wait_send())
     pl.when(g_sent)(g_out.wait_send)
     for one in (
-        g_p, g_m, g_in, gf_p, gf_m, *v_far_p, *v_far_m, *v_p, *v_m, vf_p, vf_m, e_p, e_m, e_far, v_x,
+        *g_p, *g_m, g_in, gf_p, gf_m, *v_far_p, *v_far_m, *v_p, *v_m, vf_p, vf_m, e_p, e_m, e_far, v_x,
         *give, *far, *near, *last, *sum(z_out, []),
     ):
         one.wait_send()

time: 40.1 us -> 39.5 us (0.985)
    pallas_call x1, Pallas kernels: 36.5 us -> 36.1 us  [shards(): pl.pallas_call(kernel, out_shape=(jax.ShapeDtypeStruct((6, 24, 384), F32)...]
where the time goes in v8:
time: 39.5 us; the launch traced here: 38.9 us
  Pallas kernels  36.1 us (91%)
  local copies, waits for them, and re-layouts  2.26 us (6%)
  between operations  0.64 us (2%)
    pallas_call x1, Pallas kernels, shards(): pl.pallas_call(kernel, out_shape=(jax.ShapeDtypeStruct((6, 24, 384), F32)...  36.1 us
    unnamed x2, local copies, waits for them, and re-layouts  2.26 us

profile of v8, /device:TPU:2, one launch (start us, length us, event | category | flops | bytes accessed | tf_op | source)
XLA Modules:
  0.0 38.9 jit_solution(1206307439736109774)
XLA Ops:
  0.6 36.1 %tubelet_backward.1 = (f32[6,24,384]{2,1,0:T(8,128)}, f32[24,512]{1,0:T(8,128)S(1)}) custom-call(bf16[288,384]{1,0:T(8,128)(2,1)} %bitcast.3, bf16[12,24,384]{2,1,0:T(8,128)(2,1)} %bitcast.4, bf16[2,2,32,512]{3,2,1,0:T(8,128)(2,1)} %tokens.1, bf16[3072,512]{1,0:T(8,128)(2,1)} %weight.1, bf16[1584,512]{1,0:T(8,128)(2,1)} %constant.2.clone.packed), custom_call_target="tpu_custom_call" | custom-call | tf_op jit(solution)/shard_map/tubelet_backward/pallas_call | solution.py:532
  36.7 1.6 %copy.8 = f32[3,2,24,384]{3,2,1,0:T(8,128)} copy(f32[3,2,24,384]{3,2,1,0:T(8,128)} %bitcast.5) | data formatting | bytes 442368
  38.3 0.6 %copy.9 = f32[24,512]{1,0:T(8,128)} copy(f32[24,512]{1,0:T(8,128)S(1)} %get-tuple-element.9) | data formatting | bytes 98304

commit v9 on v8

--- a/solution.py
+++ b/solution.py
@@ -182,10 +182,12 @@
     def greet(to):
         pl.semaphore_signal(barrier, inc=1, device_id=to, device_id_type=MESH)
 
-    for to in (yp, ym, {"row": (r + 4) % 8}, xp, xm, other, *zs, partner):
+    for to in (partner, *zs[::-1]):
         greet(to)
-    for there, to in near:
+    for there, to in near[::-1]:
         pl.when(there)(lambda to=to: greet(to))
+    for to in ({"row": (r + 4) % 8}, yp, ym, xp, xm, other):
+        greet(to)
 
     def one_if(p):
         return jnp.where(p, jnp.int32(1), jnp.int32(0))
@@ -518,6 +520,28 @@
         one.wait_send()
 
 
+def put_out(video_grad, weight_grad, vout, wout, held, sem):
+    parts = 3
+    arrive = [
+        pltpu.make_async_copy(video_grad.at[pl.ds(2 * k, 2)], held.at[pl.ds(2 * k, 2)], sem.at[k])
+        for k in range(parts)
+    ]
+    leave = [
+        pltpu.make_async_copy(held.at[pl.ds(2 * k, 2)], vout.at[pl.ds(2 * k, 2)], sem.at[parts + k])
+        for k in range(parts)
+    ]
+    last = pltpu.make_async_copy(weight_grad, wout, sem.at[2 * parts])
+    for one in arrive:
+        one.start()
+    last.start()
+    for a, b in zip(arrive, leave):
+        a.wait()
+        b.start()
+    for one in leave:
+        one.wait()
+    last.wait()
+
+
 def shards(video, grad_tokens, weight):
     packed = jnp.asarray(selections(), BF16)
     anywhere = pl.BlockSpec(memory_space=pltpu.HBM)
@@ -557,6 +581,18 @@
         ),
         name="tubelet_backward",
     )(video.reshape(288, 384), video.reshape(12, 24, 384), grad_tokens, weight, packed)
+    video_grad, weight_grad = pl.pallas_call(
+        put_out,
+        out_shape=(
+            jax.ShapeDtypeStruct((6, 24, 384), F32),
+            jax.ShapeDtypeStruct((24, 512), F32),
+        ),
+        in_specs=[anywhere, in_vmem],
+        out_specs=(anywhere, anywhere),
+        scratch_shapes=[v(6, 24, 384), pltpu.SemaphoreType.DMA((7,))],
+        compiler_params=pltpu.CompilerParams(vmem_limit_bytes=VMEM_BYTES),
+        name="put_out",
+    )(video_grad, weight_grad)
     return video_grad.reshape(3, 2, 24, 384), weight_grad
 
 

time: 39.5 us -> 38.9 us (0.985)
  local copies, waits for them, and re-layouts: 2.26 us -> 0 us
  Pallas kernels: 36.1 us -> 37.6 us
    unnamed x2 -> x0, local copies, waits for them, and re-layouts: 2.26 us -> none
    pallas_call x0 -> x1, Pallas kernels: none -> 1.67 us  [shards(): pl.pallas_call(put_out, out_shape=(jax.ShapeDtypeStruct((6, 24, 384), F32...]
where the time goes in v9:
time: 38.9 us; the launch traced here: 38.2 us
  Pallas kernels  37.6 us (97%)
  between operations  0.64 us (2%)
    pallas_call x1, Pallas kernels, shards(): pl.pallas_call(kernel, out_shape=(jax.ShapeDtypeStruct((6, 24, 384), F32)...  35.9 us
    pallas_call x1, Pallas kernels, shards(): pl.pallas_call(put_out, out_shape=(jax.ShapeDtypeStruct((6, 24, 384), F32...  1.67 us

profile of v9, /device:TPU:2, one launch (start us, length us, event | category | flops | bytes accessed | tf_op | source)
XLA Modules:
  0.0 38.2 jit_solution(1274144324187304130)
XLA Ops:
  0.6 35.9 %tubelet_backward.1 = (f32[6,24,384]{2,1,0:T(8,128)}, f32[24,512]{1,0:T(8,128)S(1)}) custom-call(bf16[288,384]{1,0:T(8,128)(2,1)} %bitcast.3, bf16[12,24,384]{2,1,0:T(8,128)(2,1)} %bitcast.4, bf16[2,2,32,512]{3,2,1,0:T(8,128)(2,1)} %tokens.1, bf16[3072,512]{1,0:T(8,128)(2,1)} %weight.1, bf16[1584,512]{1,0:T(8,128)(2,1)} %constant.2.clone.packed), custom_call_target="tpu_custom_call" | custom-call | tf_op jit(solution)/shard_map/tubelet_backward/pallas_call | solution.py:556
  36.6 1.7 %put_out.1 = (f32[6,24,384]{2,1,0:T(8,128)}, f32[24,512]{1,0:T(8,128)}) custom-call(f32[6,24,384]{2,1,0:T(8,128)} %get-tuple-element.6.video_grad, f32[24,512]{1,0:T(8,128)S(1)} %get-tuple-element.7.weight_grad), custom_call_target="tpu_custom_call" | custom-call | tf_op jit(solution)/shard_map/put_out/pallas_call | solution.py:584

commit v10 on v9

--- a/solution.py
+++ b/solution.py
@@ -329,6 +329,13 @@
         loads[k].wait()
     unfold(0)
 
+    g_p[0].wait_recv()
+    gf_p = remote(gbuf.at[0, 1], gbuf.at[0, 3], yp)
+    gf_p.start()
+    g_m[0].wait_recv()
+    gf_m = remote(gbuf.at[1, 2], gbuf.at[1, 3], ym)
+    gf_m.start()
+
     g_in.wait_recv()
     pl.when(g_got)(g_out.wait_recv)
     for copy, _, got in token_halo:
@@ -344,13 +351,6 @@
         pg[0, at, 64:128] = pltpu.roll(out[:, 0:128], 64, 1)[:, 64:128]
         pg[1, at, 64:128] = out[:, 64:128]
         pg[2, at, :] = out[:, 128:256]
-
-    g_p[0].wait_recv()
-    gf_p = remote(gbuf.at[0, 1], gbuf.at[0, 3], yp)
-    gf_p.start()
-    g_m[0].wait_recv()
-    gf_m = remote(gbuf.at[1, 2], gbuf.at[1, 3], ym)
-    gf_m.start()
 
     for one in v_far_p:
         one.wait_recv()

time: 38.9 us -> 38.7 us (level)
  no operation moved by 1% of the time
where the time goes in v10:
time: 38.7 us; the launch traced here: 38.4 us
  Pallas kernels  37.7 us (97%)
  between operations  0.64 us (2%)
    pallas_call x1, Pallas kernels, shards(): pl.pallas_call(kernel, out_shape=(jax.ShapeDtypeStruct((6, 24, 384), F32)...  36.1 us
    pallas_call x1, Pallas kernels, shards(): pl.pallas_call(put_out, out_shape=(jax.ShapeDtypeStruct((6, 24, 384), F32...  1.67 us

profile of v10, /device:TPU:2, one launch (start us, length us, event | category | flops | bytes accessed | tf_op | source)
XLA Modules:
  0.0 38.4 jit_solution(11865419564315442897)
XLA Ops:
  0.6 36.1 %tubelet_backward.1 = (f32[6,24,384]{2,1,0:T(8,128)}, f32[24,512]{1,0:T(8,128)S(1)}) custom-call(bf16[288,384]{1,0:T(8,128)(2,1)} %bitcast.3, bf16[12,24,384]{2,1,0:T(8,128)(2,1)} %bitcast.4, bf16[2,2,32,512]{3,2,1,0:T(8,128)(2,1)} %tokens.1, bf16[3072,512]{1,0:T(8,128)(2,1)} %weight.1, bf16[1584,512]{1,0:T(8,128)(2,1)} %constant.2.clone.packed), custom_call_target="tpu_custom_call" | custom-call | tf_op jit(solution)/shard_map/tubelet_backward/pallas_call | solution.py:556
  36.7 1.7 %put_out.1 = (f32[6,24,384]{2,1,0:T(8,128)}, f32[24,512]{1,0:T(8,128)}) custom-call(f32[6,24,384]{2,1,0:T(8,128)} %get-tuple-element.6.video_grad, f32[24,512]{1,0:T(8,128)S(1)} %get-tuple-element.7.weight_grad), custom_call_target="tpu_custom_call" | custom-call | tf_op jit(solution)/shard_map/put_out/pallas_call | solution.py:584

commit v11 on v10

--- a/solution.py
+++ b/solution.py
@@ -298,6 +298,13 @@
         one.start()
     er[0] = ex[y]
 
+    g_p[0].wait_recv()
+    gf_p = remote(gbuf.at[0, 1], gbuf.at[0, 3], yp)
+    gf_p.start()
+    g_m[0].wait_recv()
+    gf_m = remote(gbuf.at[1, 2], gbuf.at[1, 3], ym)
+    gf_m.start()
+
     def unfold(*sources):
         pixels = []
         for n in sources:
@@ -328,13 +335,6 @@
     for k in range(7, 11):
         loads[k].wait()
     unfold(0)
-
-    g_p[0].wait_recv()
-    gf_p = remote(gbuf.at[0, 1], gbuf.at[0, 3], yp)
-    gf_p.start()
-    g_m[0].wait_recv()
-    gf_m = remote(gbuf.at[1, 2], gbuf.at[1, 3], ym)
-    gf_m.start()
 
     g_in.wait_recv()
     pl.when(g_got)(g_out.wait_recv)

time: 38.7 us -> 38.7 us (level)
  no operation moved by 1% of the time
where the time goes in v11:
time: 38.7 us; the launch traced here: 38.4 us
  Pallas kernels  37.7 us (97%)
  between operations  0.64 us (2%)
    pallas_call x1, Pallas kernels, shards(): pl.pallas_call(kernel, out_shape=(jax.ShapeDtypeStruct((6, 24, 384), F32)...  36.1 us
    pallas_call x1, Pallas kernels, shards(): pl.pallas_call(put_out, out_shape=(jax.ShapeDtypeStruct((6, 24, 384), F32...  1.67 us

profile of v11, /device:TPU:2, one launch (start us, length us, event | category | flops | bytes accessed | tf_op | source)
XLA Modules:
  0.0 38.4 jit_solution(4842110783902046929)
XLA Ops:
  0.6 36.1 %tubelet_backward.1 = (f32[6,24,384]{2,1,0:T(8,128)}, f32[24,512]{1,0:T(8,128)S(1)}) custom-call(bf16[288,384]{1,0:T(8,128)(2,1)} %bitcast.3, bf16[12,24,384]{2,1,0:T(8,128)(2,1)} %bitcast.4, bf16[2,2,32,512]{3,2,1,0:T(8,128)(2,1)} %tokens.1, bf16[3072,512]{1,0:T(8,128)(2,1)} %weight.1, bf16[1584,512]{1,0:T(8,128)(2,1)} %constant.2.clone.packed), custom_call_target="tpu_custom_call" | custom-call | tf_op jit(solution)/shard_map/tubelet_backward/pallas_call | solution.py:556
  36.7 1.7 %put_out.1 = (f32[6,24,384]{2,1,0:T(8,128)}, f32[24,512]{1,0:T(8,128)}) custom-call(f32[6,24,384]{2,1,0:T(8,128)} %get-tuple-element.6.video_grad, f32[24,512]{1,0:T(8,128)S(1)} %get-tuple-element.7.weight_grad), custom_call_target="tpu_custom_call" | custom-call | tf_op jit(solution)/shard_map/put_out/pallas_call | solution.py:584
